TPU v7x, 256 devices: a whole 4x4x8 slice. The times are simulated.
256 devices in a mesh: seq: 8 (over z), tensor: 8 (over x, y_hi), dp: 4 (over y_lo, core).
Axes of the slice: x: 4, y: 4 (y_hi: 2, y_lo: 2; y = y_hi * 2 + y_lo), z: 8, core: 2. Of those that a mesh axis runs over, the one named last changes fastest.
Arguments:
- tokens: bfloat16 [4, 2048, 3072], P('dp', 'seq'), may hold values from -6 to 6
- cotangent: bfloat16 [4, 2048, 3072], P('dp', 'seq'), may hold values from -6 to 6
- qkv_weight: bfloat16 [3072, 3, 3072], P(('seq', 'dp'), None, 'tensor'), may hold values from -0.109375 to 0.109375
- out_weight: bfloat16 [3072, 3072], P(('seq', 'dp'), 'tensor'), may hold values from -0.109375 to 0.109375
Outputs:
- qkv_grad: float32 [3072, 3, 3072], P(('seq', 'dp'), None, 'tensor')
- out_grad: float32 [3072, 3072], P(('seq', 'dp'), 'tensor')
- branch_grad: bfloat16 [4, 2048, 3072], P('dp', 'seq', 'tensor')
All inputs are finite; a program needn't handle non-finite values.
Results may differ from a plain program's by a relative error of at most 0.025.
Values may be sent and summed in bfloat16 or wider, within the bound.
No kernel may reach another device: no remote copies, remote signals or barrier semaphores. Data moves between devices by JAX's collectives and lax.ppermute only.
A program may use at most 128 MiB of HBM per device.

v0:
```python
import jax
import jax.numpy as jnp
from jax import lax
from jax.experimental import pallas as pl
from jax.experimental.pallas import tpu as pltpu
from jax.sharding import PartitionSpec as P

HD = 128
epsilon = 1e-06
BF = jnp.bfloat16
F32 = jnp.float32


def dot(a, b, ca=1, cb=0):
    return lax.dot_general(a, b, (((ca,), (cb,)), ((), ())), preferred_element_type=F32)


def normalize(values, axis=-1):
    average = jnp.mean(values, axis=axis, keepdims=True)
    centered = values - average
    inverse = lax.rsqrt(jnp.mean(centered * centered, axis=axis, keepdims=True) + epsilon)
    return (centered * inverse, inverse)


def normalize_back(gradient, normed, inverse, axis=-1):
    mean_grad = jnp.mean(gradient, axis=axis, keepdims=True)
    mean_both = jnp.mean(gradient * normed, axis=axis, keepdims=True)
    return (gradient - mean_grad - normed * mean_both) * inverse


ARBITRARY = pltpu.CompilerParams(dimension_semantics=("arbitrary",))


def prepare_body(
    me_ref, tok_ref, cot_ref, unit_ref, inv_ref, xk_ref, xs_ref, xr_ref, ck_ref, cs_ref, cr_ref, mean_ref
):
    step = pl.program_id(0)
    rows = tok_ref.shape[0]
    group, _, own, _ = xk_ref.shape
    block = 4 * own
    core = me_ref[1]

    @pl.when(step == 0)
    def _():
        values = tok_ref[...].astype(F32)
        average = jnp.mean(values, axis=-1, keepdims=True)
        centered = values - average
        inverse = lax.rsqrt(jnp.mean(centered * centered, axis=-1, keepdims=True) + epsilon)
        mean_ref[...] = jnp.broadcast_to(average, (rows, HD))
        inv_ref[...] = jnp.broadcast_to(inverse, (rows, HD))

    def slab(s, carry):
        here = pl.ds(pl.multiple_of((step * group + s) * block, HD), block)
        there = pl.ds(pl.multiple_of(s * block, HD), block)
        unit = (tok_ref[:, here].astype(F32) - mean_ref[:, :1]) * inv_ref[:, :1]
        unit_ref[:, there] = unit
        for value, refs in (
            (unit.astype(BF), (xk_ref, xs_ref, xr_ref)),
            (cot_ref[:, here], (ck_ref, cs_ref, cr_ref)),
        ):
            turned = value.T

            def place(refs, turned, c):
                for y in range(2):
                    away_y = lax.rem(me_ref[2] + y, 2)
                    at = (2 * y + c) * own
                    refs[0][s, away_y] = turned[at : at + own]
                    at = (2 * y + 1 - c) * own
                    refs[1][s, away_y] = turned[at : at + own]

            @pl.when(core == 0)
            def _():
                place(refs, turned, 0)

            @pl.when(core == 1)
            def _():
                place(refs, turned, 1)

            for c in range(2):
                refs[2][s, c] = refs[c][s].reshape(2 * own, rows).T
        return carry

    lax.fori_loop(0, group, slab, 0)


def prepare(me, tokens, cotangent, slabs, steps=4):
    rows, features = tokens.shape
    own = features // slabs // 4
    group = slabs // steps
    whole = pl.BlockSpec((rows, features), lambda i, me: (0, 0))
    turned = pl.BlockSpec((group, 2, own, rows), lambda i, me: (i, 0, 0, 0))
    plain = pl.BlockSpec((group, 2, rows, 2 * own), lambda i, me: (i, 0, 0, 0))
    turned_shape = jax.ShapeDtypeStruct((slabs, 2, own, rows), BF)
    plain_shape = jax.ShapeDtypeStruct((slabs, 2, rows, 2 * own), BF)
    return pl.pallas_call(
        prepare_body,
        grid_spec=pltpu.PrefetchScalarGridSpec(
            num_scalar_prefetch=1,
            grid=(steps,),
            in_specs=[whole, whole],
            out_specs=[
                pl.BlockSpec((rows, features // steps), lambda i, me: (0, i)),
                pl.BlockSpec((rows, HD), lambda i, me: (0, 0)),
            ]
            + [turned, turned, plain] * 2,
            scratch_shapes=[pltpu.VMEM((rows, HD), F32)],
        ),
        out_shape=[
            jax.ShapeDtypeStruct((rows, features), F32),
            jax.ShapeDtypeStruct((rows, HD), F32),
        ]
        + [turned_shape, turned_shape, plain_shape] * 2,
        compiler_params=ARBITRARY,
        name="prepare",
    )(me, tokens, cotangent)


def distance(i):
    return (i + 1) // 2 * (1 if i % 2 == 0 else -1)


def far_from(i):
    return lax.div(i + 1, 2) * (1 - 2 * lax.rem(i, 2))


def project_kv_body(
    me_ref, x_ref, near_ref, near_far_ref, far_ref, far_far_ref, k_ref, kl_ref, vl_ref, acc_ref
):
    slabs = x_ref.shape[0]
    width = k_ref.shape[1]
    close = near_ref.shape[0]
    acc_ref[...] = jnp.zeros_like(acc_ref)

    def take(mine_ref, theirs_ref, first):
        def step(k, carry):
            slab = lax.rem(me_ref[0] + slabs + far_from(k + first), slabs)
            acc_ref[...] += dot(x_ref[slab, 0], mine_ref[k]) + dot(x_ref[slab, 1], theirs_ref[k])
            return carry

        lax.fori_loop(0, mine_ref.shape[0], step, 0)

    take(near_ref, near_far_ref, 0)
    take(far_ref, far_far_ref, close)
    k_ref[...] = acc_ref[:, :width]
    for at in range(0, width, HD):
        kl_ref[:, at : at + HD] = normalize(acc_ref[:, at : at + HD])[0].astype(BF)
    vl_ref[...] = acc_ref[:, width:].astype(BF)


def project_kv(me, x, near, near_far, far, far_far):
    rows, width = x.shape[2], near.shape[2] // 2
    return pl.pallas_call(
        project_kv_body,
        in_specs=[pl.BlockSpec(memory_space=pltpu.SMEM)] + [pl.BlockSpec(memory_space=pltpu.VMEM)] * 5,
        out_shape=[
            jax.ShapeDtypeStruct((rows, width), F32),
            jax.ShapeDtypeStruct((rows, width), BF),
            jax.ShapeDtypeStruct((rows, width), BF),
        ],
        scratch_shapes=[pltpu.VMEM((rows, 2 * width), F32)],
        name="project_kv",
    )(me, x, near, near_far, far, far_far)


def project_qo_body(x_ref, c_ref, b_ref, by_ref, bc_ref, byc_ref, q_ref, g_ref, acc_ref):
    slabs = x_ref.shape[0]
    width = q_ref.shape[1]
    acc_ref[...] = jnp.zeros_like(acc_ref)

    def step(k, carry):
        for left_ref, at in ((x_ref, 0), (c_ref, width)):
            cols = slice(at, at + width)
            part = 0.0
            for c, (first, second) in enumerate(((b_ref, by_ref), (bc_ref, byc_ref))):
                piece = jnp.concatenate([first[k, :, cols], second[k, :, cols]], axis=0)
                part = part + dot(left_ref[k, c], piece)
            acc_ref[:, cols] += part
        return carry

    lax.fori_loop(0, slabs, step, 0)
    q_ref[...] = acc_ref[:, :width]
    g_ref[...] = acc_ref[:, width:].astype(BF)


VMEM = pl.BlockSpec(memory_space=pltpu.VMEM)
SMEM = pl.BlockSpec(memory_space=pltpu.SMEM)


def project_qo(x, c, *pieces):
    rows, width = x.shape[2], pieces[0].shape[2] // 2
    return pl.pallas_call(
        project_qo_body,
        in_specs=[VMEM] * 6,
        out_shape=[jax.ShapeDtypeStruct((rows, width), F32), jax.ShapeDtypeStruct((rows, width), BF)],
        scratch_shapes=[pltpu.VMEM((rows, 2 * width), F32)],
        name="project_qo",
    )(x, c, *pieces)


def attend_body(me_ref, q_ref, g_ref, *refs, count):
    k_refs, v_refs = refs[:count], refs[count : 2 * count]
    att_ref, qb_ref, pair_ref, e_ref = refs[2 * count :]
    slabs = pair_ref.shape[0]
    rows = q_ref.shape[0]
    scale = HD ** (-0.5)
    q_unit, q_inv = normalize(q_ref[...])
    q = q_unit.astype(BF)
    g = g_ref[...]
    total = jnp.zeros((8, rows), F32)
    att_t = jnp.zeros((HD, rows), F32)
    at = 0
    spots = []
    for k_ref, v_ref in zip(k_refs, v_refs):
        keys = k_ref.shape[0]
        here = slice(at, at + keys)
        spots.append(here)
        at += keys
        e = jnp.exp(dot(k_ref[...], q, 1, 1) * scale)
        e_ref[here] = e
        total = total + jnp.sum(e.reshape(keys // 8, 8, rows), axis=0)
        att_t = att_t + dot(v_ref[...].T, e.astype(BF))
    total = jnp.sum(total, axis=0, keepdims=True)
    inv_total = 1.0 / total
    att = (att_t * inv_total).T.astype(BF)
    att_ref[...] = att
    delta = jnp.sum((g.astype(F32) * att.astype(F32)).T, axis=0, keepdims=True)
    dq_t = jnp.zeros((HD, rows), F32)
    for i, (k_ref, v_ref, here) in enumerate(zip(k_refs, v_refs, spots)):
        p = e_ref[here] * inv_total
        dp = dot(v_ref[...], g, 1, 1)
        ds = (p * ((dp - delta) * scale)).astype(BF)
        slab = lax.rem(me_ref[0] + slabs + distance(i), slabs)
        pair_ref[slab, 0] = dot(ds, q).astype(BF)
        pair_ref[slab, 1] = dot(p.astype(BF), g).astype(BF)
        dq_t = dq_t + dot(k_ref[...].T, ds)
    qb_ref[...] = normalize_back(dq_t.T, q_unit, q_inv).astype(BF)


def attend(me, q, g, keys, values):
    rows, width = q.shape
    sizes = [k.shape[0] for k in keys]
    shape = (sum(sizes) // rows, 2, rows, width)
    row_spec = pl.BlockSpec((rows, HD), lambda h, me: (0, h))
    specs = [pl.BlockSpec((n, HD), lambda h, me: (0, h)) for n in sizes]
    return pl.pallas_call(
        lambda *refs: attend_body(*refs, count=len(sizes)),
        grid_spec=pltpu.PrefetchScalarGridSpec(
            num_scalar_prefetch=1,
            grid=(width // HD,),
            in_specs=[row_spec, row_spec] + specs * 2,
            out_specs=[
                row_spec,
                row_spec,
                pl.BlockSpec((*shape[:3], HD), lambda h, me: (0, 0, 0, h)),
            ],
            scratch_shapes=[pltpu.VMEM((sum(sizes), rows), F32)],
        ),
        out_shape=[
            jax.ShapeDtypeStruct((rows, width), BF),
            jax.ShapeDtypeStruct((rows, width), BF),
            jax.ShapeDtypeStruct(shape, BF),
        ],
        compiler_params=ARBITRARY,
        name="attend",
    )(me, q, g, *keys, *values)


def terms_of(x_ref, c_ref, a_ref, b_ref, store):
    slabs, _, own, rows = x_ref.shape
    width = a_ref.shape[1]

    def step(k, carry):
        spots = [2 * k + i for i in range(2)]
        for left_ref, right_ref, cols in (
            (x_ref, a_ref, slice(None, width)),
            (c_ref, b_ref, slice(width, None)),
        ):
            left = jnp.concatenate([left_ref[spot].reshape(2 * own, rows) for spot in spots], axis=0)
            value = dot(left, right_ref[...])
            for i in range(2):
                for y in range(2):
                    at = (2 * i + y) * own
                    store(2 * k + i, y, cols, value[at : at + own])
        return carry

    lax.fori_loop(0, slabs // 2, step, 0)


def query_send_body(x_ref, c_ref, a_ref, b_ref, out_ref):
    def store(r, y, cols, value):
        out_ref[y, r, :, cols] = value.astype(BF)

    terms_of(x_ref, c_ref, a_ref, b_ref, store)


def query_keep_body(x_ref, c_ref, a_ref, b_ref, got_ref, stay_ref, go_ref):
    def store(r, y, cols, value):
        (stay_ref, go_ref)[y][r, :, cols] = (value + got_ref[y, r, :, cols].astype(F32)).astype(BF)

    terms_of(x_ref, c_ref, a_ref, b_ref, store)


def key_send_body(x_ref, k_ref, sum_ref, kb_ref, vb_ref, out_ref):
    width = k_ref.shape[1]
    rows = k_ref.shape[0]
    for h in range(width // HD):
        cols = slice(h * HD, (h + 1) * HD)
        unit, inv = normalize(k_ref[:, cols])
        kb_ref[:, cols] = normalize_back(sum_ref[:rows, cols].astype(F32), unit, inv).astype(BF)
    vb_ref[...] = sum_ref[rows:]

    def store(r, y, cols, value):
        out_ref[r, y, :, cols] = value.astype(BF)

    terms_of(x_ref, x_ref, kb_ref, vb_ref, store)


def key_keep_body(x_ref, a_ref, b_ref, got_ref, stay_ref, y_ref, out_ref):
    own = x_ref.shape[2]

    def store(r, y, cols, value):
        total = value + got_ref[r, y, :, cols].astype(F32)
        out_ref[r, (1 + y) * own : (2 + y) * own, cols] = total.astype(BF)

    terms_of(x_ref, x_ref, a_ref, b_ref, store)
    for r in range(x_ref.shape[0]):
        out_ref[r, :own] = (stay_ref[r].astype(F32) + y_ref[r].astype(F32)).astype(BF)


def call(body, shapes, *operands):
    return pl.pallas_call(
        body,
        in_specs=[VMEM] * len(operands),
        out_shape=[jax.ShapeDtypeStruct(v, BF) for v in shapes],
    )(*operands)


def inner_body(
    me_ref, qb_ref, kb_ref, vb_ref, near_ref, near_far_ref, far_ref, far_far_ref,
    *refs, close,
):
    step = pl.program_id(0)
    qo_refs, (unit_ref, out_ref, sum_ref, both_ref, w_ref) = refs[:4], refs[4:]
    own = qo_refs[0].shape[1]
    width = qb_ref.shape[1]
    away_y, away_c = me_ref[2], me_ref[1]

    def place(refs):
        for c, ref in enumerate(refs):
            for y in range(2):
                spot = lax.rem(away_y + y, 2), lax.rem(away_c + c, 2)
                w_ref[spot[0], spot[1], :, :width] = qo_refs[2 * c + y][0, :, :width]
                w_ref[spot[0], spot[1], :, width:] = ref[0, y * own : (y + 1) * own]

    @pl.when(step < close)
    def _():
        place((near_ref, near_far_ref))

    @pl.when(step >= close)
    def _():
        place((far_ref, far_far_ref))

    low = jnp.concatenate([qb_ref[...], kb_ref[...], vb_ref[...]], axis=1)
    result = dot(low, w_ref[...].reshape(4 * own, 3 * width), 1, 1)
    out_ref[0] = result.astype(BF)
    both = result * unit_ref[...]
    lanes = range(0, result.shape[1], HD)
    plain = sum(result[:, i : i + HD] for i in lanes)
    times = sum(both[:, i : i + HD] for i in lanes)

    @pl.when(step == 0)
    def _():
        sum_ref[...] = plain
        both_ref[...] = times

    @pl.when(step > 0)
    def _():
        sum_ref[...] += plain
        both_ref[...] += times


def inner(me, qb, kb, vb, near, near_far, far, far_far, pieces, unit):
    rows, width = qb.shape
    _, own, both = pieces[0].shape
    close = near.shape[0]
    slabs = close + far.shape[0]

    def place(i, me):
        sign = 1 - 2 * lax.rem(i, 2)
        return lax.rem(me[0] + slabs + lax.div(i + 1, 2) * sign, slabs)

    whole = pl.BlockSpec((rows, width), lambda i, me: (0, 0))
    stat = pl.BlockSpec((rows, HD), lambda i, me: (0, 0))

    def first(rows):
        return pl.BlockSpec((1, rows, both), lambda i, me: (jnp.minimum(i, close - 1), 0, 0))

    def last(rows):
        return pl.BlockSpec((1, rows, both), lambda i, me: (jnp.maximum(i - close, 0), 0, 0))

    return pl.pallas_call(
        lambda *refs: inner_body(*refs, close=close),
        grid_spec=pltpu.PrefetchScalarGridSpec(
            num_scalar_prefetch=1,
            grid=(slabs,),
            in_specs=[whole] * 3
            + [first(2 * own)] * 2
            + [last(2 * own)] * 2
            + [pl.BlockSpec((1, own, both), lambda i, me: (place(i, me), 0, 0))] * 4
            + [pl.BlockSpec((rows, 4 * own), lambda i, me: (0, place(i, me)))],
            out_specs=[
                pl.BlockSpec((1, rows, 4 * own), lambda i, me: (place(i, me), 0, 0)),
                stat,
                stat,
            ],
            scratch_shapes=[pltpu.VMEM((2, 2, own, 3 * width), BF)],
        ),
        out_shape=[
            jax.ShapeDtypeStruct((slabs, rows, 4 * own), BF),
            jax.ShapeDtypeStruct((rows, HD), F32),
            jax.ShapeDtypeStruct((rows, HD), F32),
        ],
        compiler_params=ARBITRARY,
        name="inner",
    )(me, qb, kb, vb, near, near_far, far, far_far, *pieces, unit)


def swap(value, axis):
    return lax.ppermute(value, axis, [(0, 1), (1, 0)])


def turns():
    size = lax.axis_size("seq")
    return [(i, (i + 1) % size) for i in range(size)], [(i, (i - 1) % size) for i in range(size)]


def ring_gather(value, held=None, last=None):
    up, down = turns()
    half = value.shape[0] // 2
    rows = [value]
    high = low = value
    for step in range(len(up) // 2 - 1):
        high = lax.ppermute(high, "seq", up)
        low = lax.ppermute(low, "seq", down)
        if step == 0 and held is not None:
            high, low, held = lax.optimization_barrier((high, low, held))
        rows += [high, low]
    if last is None:
        rows.append(lax.ppermute(high[:half], "seq", up))
        rows.append(lax.ppermute(low[half:], "seq", down))
    else:
        rows.append(lax.ppermute(high, "seq", up) if last else lax.ppermute(low, "seq", down))
    return rows if held is None else (rows, held)


def whole(ring):
    return ring[:-2] + [jnp.concatenate(ring[-2:], axis=0)]


def pieces_of(value):
    parts = []
    for _ in range(3):
        part = lax.reduce_precision(value, 8, 7)
        parts.append(part.astype(BF))
        value = value - part
    return parts


def layer(tokens, cotangent, qkv_weight, out_weight):
    row_count, feature_count = tokens.shape[1:]
    own, _, width = qkv_weight.shape
    slabs = lax.axis_size("seq")
    shares = lax.axis_size(("x", "yhi"))
    me = jnp.stack([lax.axis_index("seq"), lax.axis_index("core"), lax.axis_index("ylo")]).astype(jnp.int32)
    kv_weight = qkv_weight[:, 1:].reshape(own, 2 * width)
    qo_weight = jnp.concatenate([qkv_weight[:, 0], out_weight], axis=1)
    qo_mine = lax.all_gather(qo_weight, "seq")
    kv_weight = jnp.concatenate([kv_weight, swap(kv_weight, "ylo")], axis=0)
    unit, inverse, *turned = prepare(me, tokens[0], cotangent[0], slabs)
    x_keep, x_send, x_r, c_keep, c_send, c_r = turned
    ring, x_r = ring_gather(kv_weight, x_r)
    ring = whole(ring)
    near, far = jnp.stack(ring[:5]), jnp.stack(ring[5:])
    near_far, far_far = swap(near, "core"), swap(far, "core")
    qo_y = swap(qo_mine, "ylo")
    key, key_low, value_low = project_kv(me, x_r, near, near_far, far, far_far)
    keys = ring_gather(key_low, last=True)
    values = ring_gather(value_low, last=False)
    qo_pieces = (qo_mine, qo_y, swap(qo_mine, "core"), swap(qo_y, "core"))
    query, grad_rows = project_qo(x_r, c_r, *qo_pieces)
    attended, query_back, pair = attend(me, query, grad_rows, keys, values)
    pair = lax.psum_scatter(
        pair.reshape(slabs * 2 * row_count, width), "seq", scatter_dimension=0, tiled=True
    )
    both = 2 * width
    got = swap(call(query_send_body, [(2, slabs, own, both)], x_send, c_send, query_back, attended)[0], "core")
    stay, go = call(query_keep_body, [(slabs, own, both)] * 2, x_keep, c_keep, query_back, attended, got)
    from_y = swap(go, "ylo")
    key, from_y = lax.optimization_barrier((key, from_y))
    key_grad, value_grad, send = call(
        key_send_body, [(row_count, width)] * 2 + [(slabs, 2, own, both)], x_send, key, pair
    )
    merged = call(
        key_keep_body,
        [(slabs, 3 * own, both)],
        x_keep, key_grad, value_grad, swap(send, "core"), stay, from_y,
    )[0]
    merged, key_grad = lax.optimization_barrier((merged, key_grad))
    merged = lax.psum_scatter(
        merged.reshape(slabs * 3 * own, both), "seq", scatter_dimension=0, tiled=True
    )
    query_out = merged[:own].astype(F32)
    key_value_grad = merged[own : 2 * own].astype(F32) + swap(merged[2 * own :], "ylo").astype(F32)
    share, plain, both = inner(
        me, query_back, key_grad, value_grad, near, near_far, far, far_far, qo_pieces, unit
    )
    stats = jnp.stack(pieces_of(jnp.sum(plain, axis=1)) + pieces_of(jnp.sum(both, axis=1)))
    stats = stats.reshape(-1, share.shape[2])
    stats = jnp.pad(stats, ((0, 16 - stats.shape[0]), (0, 0)))
    load = jnp.concatenate([share, jnp.broadcast_to(stats, (shares, *stats.shape))], axis=1)
    load = lax.all_to_all(load, ("x", "yhi"), 0, 0, tiled=True)
    load = load.astype(F32)
    load = jnp.sum(load, axis=0)
    own_share = load[:row_count]
    totals = load[row_count:].reshape(-1)[: 6 * row_count].reshape(2, 3, row_count)
    totals = jnp.sum(totals, axis=1)[:, :, None] / feature_count
    offset = lax.axis_index(("x", "yhi")) * share.shape[2]
    unit_own = lax.dynamic_slice_in_dim(unit, offset, share.shape[2], 1)
    branch = (own_share - totals[0] - unit_own * totals[1]) * inverse[:, :1]
    qkv_grad = jnp.stack(
        [query_out[:, :width], key_value_grad[:, :width], key_value_grad[:, width:]], axis=1
    )
    return (qkv_grad, query_out[:, width:], branch.astype(BF)[None])


def solution(mesh):
    split = jax.sharding.Mesh(
        mesh.devices.reshape(mesh.shape["seq"], mesh.shape["tensor"] // 2, 2, 2, 2),
        ("seq", "x", "yhi", "ylo", "core"),
    )
    blocks = ("seq", "ylo", "core")
    heads = ("x", "yhi")
    return jax.shard_map(
        layer,
        mesh=split,
        in_specs=(
            P(("ylo", "core"), "seq", None),
            P(("ylo", "core"), "seq", None),
            P(blocks, None, heads),
            P(blocks, heads),
        ),
        out_specs=(
            P(blocks, None, heads),
            P(blocks, heads),
            P(("ylo", "core"), "seq", heads),
        ),
        check_vma=False,
    )
```

profile of v0, /device:TPU:16, one launch (start us, length us, event | category | flops | bytes accessed | tf_op | source)
XLA Modules:
  0.0 268.5 jit_solution(5566969340890314294)
XLA Ops:
  12.1 4.3 %collective-permute-done = bf16[96,768]{1,0:T(8,128)(2,1)S(1)} collective-permute-done((bf16[96,768]{1,0:T(8,128)(2,1)S(1)}, bf16[96,768]{1,0:T(8,128)(2,1)S(1)}, u32[]{:S(2)}, u32[]{:S(2)}) %collective-permute-start) | collective-permute-done | bytes 147488 | tf_op jit(solution)/shard_map/ppermute | solution.py:429
  16.4 5.9 %collective-permute-start.2 = (bf16[192,768]{1,0:T(8,128)(2,1)S(1)}, bf16[192,768]{1,0:T(8,128)(2,1)S(1)}, u32[]{:S(2)}, u32[]{:S(2)}) collective-permute-start(bf16[192,768]{1,0:T(8,128)(2,1)S(1)} %constant_dynamic-update-slice_fusion), channel_id=1, source_target_pairs={{0,224},{32,0},{64,32},{96,64},{128,96},{160,128},{192,160},{224,1... | collective-permute-start | bytes 884744 | tf_op jit(solution)/shard_map/ppermute | solution.py:444
  22.9 9.9 %prepare.1 = (f32[256,3072]{1,0:T(8,128)}, f32[256,128]{1,0:T(8,128)}, bf16[8,2,96,256]{3,2,1,0:T(8,128)(2,1)}, bf16[8,2,96,256]{3,2,1,0:T(8,128)(2,1)}, bf16[8,...) custom-call(s32[3]{0:T(128)} %pad_add_fusion.me_ref.refs_0_, ...), custom_call_target="tpu_custom_call" | custom-call | tf_op jit(solution)/shard_map/prepare/pallas_call | solution.py:95
  34.5 3.2 %collective-permute-start.4 = (bf16[192,768]{1,0:T(8,128)(2,1)S(1)}, bf16[192,768]{1,0:T(8,128)(2,1)S(1)}, u32[]{:S(2)}, u32[]{:S(2)}) collective-permute-start(bf16[192,768]{1,0:T(8,128)(2,1)S(1)} %collective-permute-done.2), channel_id=1, source_target_pairs={{0,224},{32,0},{64,32},{96,64},{128,96},{160,128},{192,160},{224,1... | collective-permute-start | bytes 884744 | tf_op jit(solution)/shard_map/ppermute | solution.py:444
  37.8 9.8 %collective-permute-done.3 = bf16[192,768]{1,0:T(8,128)(2,1)} collective-permute-done((bf16[192,768]{1,0:T(8,128)(2,1)S(1)}, bf16[192,768]{1,0:T(8,128)(2,1)}, u32[]{:S(2)}, u32[]{:S(2)}) %collective-permute-start.3) | collective-permute-done | bytes 294944 | tf_op jit(solution)/shard_map/ppermute | solution.py:443
  47.6 3.2 %collective-permute-start.7 = (bf16[192,768]{1,0:T(8,128)(2,1)S(1)}, bf16[192,768]{1,0:T(8,128)(2,1)S(1)}, u32[]{:S(2)}, u32[]{:S(2)}) collective-permute-start(bf16[192,768]{1,0:T(8,128)(2,1)S(1)} %collective-permute-done.4), channel_id=1, source_target_pairs={{0,224},{32,0},{64,32},{96,64},{128,96},{160,128},{192,160},{224,1... | collective-permute-start | bytes 884744 | tf_op jit(solution)/shard_map/ppermute | solution.py:444
  56.2 3.3 %collective-permute-start.9 = (bf16[96,768]{1,0:T(8,128)(2,1)S(1)}, bf16[96,768]{1,0:T(8,128)(2,1)S(1)}, u32[]{:S(2)}, u32[]{:S(2)}) collective-permute-start(bf16[96,768]{1,0:T(8,128)(2,1)S(1)} %slice.70), channel_id=1, source_target_pairs={{0,224},{32,0},{64,32},{96,64},{128,96},{160,128},{192,160},{224,1... | collective-permute-start | bytes 442376 | tf_op jit(solution)/shard_map/ppermute | solution.py:450
  59.5 3.0 %collective-permute-done.8 = bf16[96,768]{1,0:T(8,128)(2,1)S(1)} collective-permute-done((bf16[96,768]{1,0:T(8,128)(2,1)S(1)}, bf16[96,768]{1,0:T(8,128)(2,1)S(1)}, u32[]{:S(2)}, u32[]{:S(2)}) %collective-permute-start.8) | collective-permute-done | bytes 147488 | tf_op jit(solution)/shard_map/ppermute | solution.py:449
  64.3 16.3 %collective-permute-done.11.by_ref.refs_9_ = bf16[8,96,768]{2,1,0:T(8,128)(2,1)} collective-permute-done((bf16[8,96,768]{2,1,0:T(8,128)(2,1)}, bf16[8,96,768]{2,1,0:T(8,128)(2,1)}, u32[]{:S(2)}, u32[]{:S(2)}) %collective-permute-start.11) | collective-permute-done | bytes 1179680 | tf_op jit(solution)/shard_map/ppermute | solution.py:429
  81.6 7.0 %project_kv.1 = (f32[256,384]{1,0:T(8,128)}, bf16[256,384]{1,0:T(8,128)(2,1)}, bf16[256,384]{1,0:T(8,128)(2,1)}) custom-call(s32[3]{0:T(128)} %pad_add_fusion.me_ref.refs_0_, bf16[8,2,256,192]{3,2,1,0:T(8,128)(2,1)} %get-tuple-element.37.x_ref, bf16[5,192,768]{2,1,0:T(8,128)(2,1)} %copy-done.1, ...), custom_call_target="tpu_custom_call" | custom-call | tf_op jit(solution)/shard_map/project_kv/pallas_call | solution.py:152
  92.3 4.4 %collective-permute-done.15.refs_5_ = bf16[256,384]{1,0:T(8,128)(2,1)S(1)} collective-permute-done((bf16[256,384]{1,0:T(8,128)(2,1)}, bf16[256,384]{1,0:T(8,128)(2,1)S(1)}, u32[]{:S(2)}, u32[]{:S(2)}) %collective-permute-start.15) | collective-permute-done | bytes 196640 | tf_op jit(solution)/shard_map/ppermute | solution.py:444
  97.5 2.4 collective-permute-start.17
  100.9 3.4 %collective-permute-done.21.refs_12_ = bf16[256,384]{1,0:T(8,128)(2,1)S(1)} collective-permute-done((bf16[256,384]{1,0:T(8,128)(2,1)}, bf16[256,384]{1,0:T(8,128)(2,1)S(1)}, u32[]{:S(2)}, u32[]{:S(2)}) %collective-permute-start.21) | collective-permute-done | bytes 196640 | tf_op jit(solution)/shard_map/ppermute | solution.py:443
  106.3 2.4 collective-permute-done.16.refs_6_
  114.6 2.1 collective-permute-done.18.refs_8_
  117.4 3.2 %collective-permute-start.27 = (bf16[256,384]{1,0:T(8,128)(2,1)S(1)}, bf16[256,384]{1,0:T(8,128)(2,1)S(1)}, u32[]{:S(2)}, u32[]{:S(2)}) collective-permute-start(bf16[256,384]{1,0:T(8,128)(2,1)S(1)} %collective-permute-done.26.refs_17_), channel_id=1, source_target_pairs={{0,224},{32,0},{64,32},{96,64},{128,96},{160,128},{192,160},{224,1... | collective-permute-start | bytes 589832 | tf_op jit(solution)/shard_map/ppermute | solution.py:452
  120.7 7.9 %project_qo.1 = (f32[256,384]{1,0:T(8,128)}, bf16[256,384]{1,0:T(8,128)(2,1)}) custom-call(bf16[8,2,256,192]{3,2,1,0:T(8,128)(2,1)} %get-tuple-element.37.x_ref, bf16[8,2,256,192]{3,2,1,0:T(8,128)(2,1)} %get-tuple-element.42.c_ref, bf16[8,96,768]{2,1,0:T(8,128)(2,1)} %bitcast.41, bf16[8,96,768]{2,1,0:T(8,128)(2,1)} %collective-permute-done.11.by_ref.refs_9_, ...), custom_call_target="tpu_custom_call" | custom-call | tf_op jit(solution)/shard_map/project_qo/pallas_call | solution.py:191
  129.5 11.7 %attend.1 = (bf16[256,384]{1,0:T(8,128)(2,1)}, bf16[256,384]{1,0:T(8,128)(2,1)}, bf16[8,2,256,384]{3,2,1,0:T(8,128)(2,1)}) custom-call(s32[3]{0:T(128)} %pad_add_fusion.me_ref.refs_0_, f32[256,384]{1,0:T(8,128)} %get-tuple-element.43.refs_1_, bf16[256,384]{1,0:T(8,128)(2,1)} %get-tuple-element.44.refs_2_, bf16[256,384]{1,0:T(8,128)(2,1)} %get-tuple-element.45.refs_3_, ...), custom_call_target="tpu_custom_call" | custom-call | tf_op jit(solution)/shard_map/attend/pallas_call | solution.py:245
  141.2 4.3 %shard_map.67 = bf16[2,8,96,768]{3,2,1,0:T(8,128)(2,1)} custom-call(bf16[8,2,96,256]{3,2,1,0:T(8,128)(2,1)} %get-tuple-element.35.x_ref, bf16[8,2,96,256]{3,2,1,0:T(8,128)(2,1)} %get-tuple-element.49.c_ref, bf16[256,384]{1,0:T(8,128)(2,1)} %get-tuple-element.47.a_ref.refs_1_, bf16[256,384]{1,0:T(8,128)(2,1)} %get-tuple-element.48.b_ref), custom_call_target="tpu_custom_call" | custom-call | tf_op jit(solution)/shard_map/pallas_call | solution.py:331
  145.6 4.7 %collective-permute-done.28.got_ref = bf16[2,8,96,768]{3,2,1,0:T(8,128)(2,1)S(1)} collective-permute-done((bf16[2,8,96,768]{3,2,1,0:T(8,128)(2,1)}, bf16[2,8,96,768]{3,2,1,0:T(8,128)(2,1)S(1)}, u32[]{:S(2)}, u32[]{:S(2)}) %collective-permute-start.28) | collective-permute-done | bytes 2359328 | tf_op jit(solution)/shard_map/ppermute | solution.py:429
  151.7 5.2 %shard_map.68 = (bf16[8,96,768]{2,1,0:T(8,128)(2,1)}, bf16[8,96,768]{2,1,0:T(8,128)(2,1)}) custom-call(bf16[8,2,96,256]{3,2,1,0:T(8,128)(2,1)} %get-tuple-element.34.x_ref, bf16[8,2,96,256]{3,2,1,0:T(8,128)(2,1)} %get-tuple-element.41.c_ref, bf16[256,384]{1,0:T(8,128)(2,1)} %get-tuple-element.47.a_ref.refs_1_, bf16[256,384]{1,0:T(8,128)(2,1)} %get-tuple-element.48.b_ref, ...), custom_call_target="tpu_custom_call" | custom-call | tf_op jit(solution)/shard_map/pallas_call | solution.py:331
  158.4 26.8 %collective-permute-done.29.y_ref = bf16[8,96,768]{2,1,0:T(8,128)(2,1)S(1)} collective-permute-done((bf16[8,96,768]{2,1,0:T(8,128)(2,1)}, bf16[8,96,768]{2,1,0:T(8,128)(2,1)S(1)}, u32[]{:S(2)}, u32[]{:S(2)}) %collective-permute-start.29) | collective-permute-done | bytes 1179680 | tf_op jit(solution)/shard_map/ppermute | solution.py:429
  185.2 2.0 reduce-scatter.3.cloned.1.call-done.sum_ref
  187.1 4.9 %shard_map.69 = (bf16[256,384]{1,0:T(8,128)(2,1)}, bf16[256,384]{1,0:T(8,128)(2,1)}, bf16[8,2,96,768]{3,2,1,0:T(8,128)(2,1)}) custom-call(bf16[8,2,96,256]{3,2,1,0:T(8,128)(2,1)} %get-tuple-element.35.x_ref, f32[256,384]{1,0:T(8,128)} %get-tuple-element.51.k_ref, bf16[512,384]{1,0:T(8,128)(2,1)} %reduce-scatter.3.cloned.1.call-done.sum_ref), custom_call_target="tpu_custom_call" | custom-call | tf_op jit(solution)/shard_map/pallas_call | solution.py:331
  192.0 4.7 %collective-permute-done.30.got_ref = bf16[8,2,96,768]{3,2,1,0:T(8,128)(2,1)S(1)} collective-permute-done((bf16[8,2,96,768]{3,2,1,0:T(8,128)(2,1)}, bf16[8,2,96,768]{3,2,1,0:T(8,128)(2,1)S(1)}, u32[]{:S(2)}, u32[]{:S(2)}) %collective-permute-start.30) | collective-permute-done | bytes 2359328 | tf_op jit(solution)/shard_map/ppermute | solution.py:429
  198.2 6.3 %shard_map.70 = bf16[8,288,768]{2,1,0:T(8,128)(2,1)} custom-call(bf16[8,2,96,256]{3,2,1,0:T(8,128)(2,1)} %get-tuple-element.34.x_ref, bf16[256,384]{1,0:T(8,128)(2,1)} %get-tuple-element.59.a_ref.refs_2_, bf16[256,384]{1,0:T(8,128)(2,1)} %get-tuple-element.54.b_ref.refs_3_, bf16[8,2,96,768]{3,2,1,0:T(8,128)(2,1)} %copy-done.5, ...), custom_call_target="tpu_custom_call" | custom-call | tf_op jit(solution)/shard_map/pallas_call | solution.py:331
  204.5 10.9 %inner.1 = (bf16[8,256,384]{2,1,0:T(8,128)(2,1)}, f32[256,128]{1,0:T(8,128)}, f32[256,128]{1,0:T(8,128)}) custom-call(s32[3]{0:T(128)} %pad_add_fusion.me_ref.refs_0_, bf16[256,384]{1,0:T(8,128)(2,1)} %get-tuple-element.47.a_ref.refs_1_, bf16[256,384]{1,0:T(8,128)(2,1)} %get-tuple-element.59.a_ref.refs_2_, bf16[256,384]{1,0:T(8,128)(2,1)} %get-tuple-element.54.b_ref.refs_3_, ...), custom_call_target="tpu_custom_call" | custom-call | tf_op jit(solution)/shard_map/inner/pallas_call | solution.py:401
  217.5 2.8 %pad_maximum_fusion = bf16[8,272,384]{2,1,0:T(8,128)(2,1)} fusion(bf16[8,16,384]{2,1,0:T(8,128)(2,1)S(1)} %broadcast_in_dim.7, bf16[8,256,384]{2,1,0:T(8,128)(2,1)} %get-tuple-element.61), kind=kLoop, calls=%fused_computation.1 | loop fusion | flops 3342336 | bytes 3342336 | tf_op jit(solution)/shard_map/concatenate | solution.py:520
  220.3 7.4 %all-to-all-start = ((bf16[8,272,384]{2,1,0:T(8,128)(2,1)}), bf16[8,272,384]{2,1,0:T(8,128)(2,1)S(1)}, u32[]{:S(2)}, u32[]{:S(2)}) async-start(bf16[8,272,384]{2,1,0:T(8,128)(2,1)} %pad_maximum_fusion), calls=%async_computation.2 | async-start | bytes 3342336 | tf_op jit(solution)/shard_map/all_to_all | solution.py:521
  227.8 24.0 %all-to-all-done = bf16[8,272,384]{2,1,0:T(8,128)(2,1)S(1)} async-done(((bf16[8,272,384]{2,1,0:T(8,128)(2,1)}), bf16[8,272,384]{2,1,0:T(8,128)(2,1)S(1)}, u32[]{:S(2)}, u32[]{:S(2)}) %all-to-all-start) | async-done | bytes 1671200 | tf_op jit(solution)/shard_map/all_to_all | solution.py:521
  252.1 1.9 fusion.3
  256.9 3.3 %collective-permute-done.31 = bf16[96,768]{1,0:T(8,128)(2,1)S(1)} collective-permute-done((bf16[96,768]{1,0:T(8,128)(2,1)S(1)}, bf16[96,768]{1,0:T(8,128)(2,1)S(1)}, u32[]{:S(2)}, u32[]{:S(2)}) %collective-permute-start.31) | collective-permute-done | bytes 147488 | tf_op jit(solution)/shard_map/ppermute | solution.py:429
  (135 shorter events, 41.7 us)
Async XLA Ops:
  7.2 46.3 %all-gather.3.cloned.1.call-start = ((), (), s32[]{:S(2)}) async-start(), calls=%async_computation.5 | async-start | bytes 1327104 | tf_op jit(solution)/shard_map/all_gather | solution.py:477
  9.7 177.5 %reduce-scatter.3.cloned.1.call-start = ((), (), s32[]{:S(2)}) async-start(), calls=%async_computation.3 | async-start | bytes 3538944 | tf_op jit(solution)/shard_map/reduce_scatter | solution.py:492
  16.4 16.5 %collective-permute-start.2 = (bf16[192,768]{1,0:T(8,128)(2,1)S(1)}, bf16[192,768]{1,0:T(8,128)(2,1)S(1)}, u32[]{:S(2)}, u32[]{:S(2)}) collective-permute-start(bf16[192,768]{1,0:T(8,128)(2,1)S(1)} %constant_dynamic-update-slice_fusion), channel_id=1, source_target_pairs={{0,224},{32,0},{64,32},{96,64},{128,96},{160,128},{192,160},{224,1... | collective-permute-start | bytes 884744 | tf_op jit(solution)/shard_map/ppermute | solution.py:444
  22.3 12.2 %collective-permute-start.1 = (bf16[192,768]{1,0:T(8,128)(2,1)S(1)}, bf16[192,768]{1,0:T(8,128)(2,1)S(1)}, u32[]{:S(2)}, u32[]{:S(2)}) collective-permute-start(bf16[192,768]{1,0:T(8,128)(2,1)S(1)} %constant_dynamic-update-slice_fusion), channel_id=1, source_target_pairs={{0,32},{32,64},{64,96},{96,128},{128,160},{160,192},{192,224},{224... | collective-permute-start | bytes 884744 | tf_op jit(solution)/shard_map/ppermute | solution.py:443
  34.5 13.1 %collective-permute-start.3 = (bf16[192,768]{1,0:T(8,128)(2,1)S(1)}, bf16[192,768]{1,0:T(8,128)(2,1)}, u32[]{:S(2)}, u32[]{:S(2)}) collective-permute-start(bf16[192,768]{1,0:T(8,128)(2,1)S(1)} %collective-permute-done.1), channel_id=1, source_target_pairs={{0,32},{32,64},{64,96},{96,128},{128,160},{160,192},{192,224},{224... | collective-permute-start | bytes 884744 | tf_op jit(solution)/shard_map/ppermute | solution.py:443
  34.5 13.1 %collective-permute-start.4 = (bf16[192,768]{1,0:T(8,128)(2,1)S(1)}, bf16[192,768]{1,0:T(8,128)(2,1)S(1)}, u32[]{:S(2)}, u32[]{:S(2)}) collective-permute-start(bf16[192,768]{1,0:T(8,128)(2,1)S(1)} %collective-permute-done.2), channel_id=1, source_target_pairs={{0,224},{32,0},{64,32},{96,64},{128,96},{160,128},{192,160},{224,1... | collective-permute-start | bytes 884744 | tf_op jit(solution)/shard_map/ppermute | solution.py:444
  47.6 8.5 %collective-permute-start.6 = (bf16[192,768]{1,0:T(8,128)(2,1)}, bf16[192,768]{1,0:T(8,128)(2,1)S(1)}, u32[]{:S(2)}, u32[]{:S(2)}) collective-permute-start(bf16[192,768]{1,0:T(8,128)(2,1)} %collective-permute-done.3), channel_id=1, source_target_pairs={{0,32},{32,64},{64,96},{96,128},{128,160},{160,192},{192,224},{224... | collective-permute-start | bytes 884744 | tf_op jit(solution)/shard_map/ppermute | solution.py:443
  47.6 8.6 %collective-permute-start.7 = (bf16[192,768]{1,0:T(8,128)(2,1)S(1)}, bf16[192,768]{1,0:T(8,128)(2,1)S(1)}, u32[]{:S(2)}, u32[]{:S(2)}) collective-permute-start(bf16[192,768]{1,0:T(8,128)(2,1)S(1)} %collective-permute-done.4), channel_id=1, source_target_pairs={{0,224},{32,0},{64,32},{96,64},{128,96},{160,128},{192,160},{224,1... | collective-permute-start | bytes 884744 | tf_op jit(solution)/shard_map/ppermute | solution.py:444
  51.9 29.8 %collective-permute-start.5 = (bf16[5,192,768]{2,1,0:T(8,128)(2,1)S(1)}, bf16[5,192,768]{2,1,0:T(8,128)(2,1)}, u32[]{:S(2)}, u32[]{:S(2)}) collective-permute-start(bf16[5,192,768]{2,1,0:T(8,128)(2,1)S(1)} %bitcast_dynamic-update-slice_fusion.near_ref.refs_4_), channel_id=1, source_target_pairs={{0,1},{1,0},{2,3},{3,2},{4,5},{5,4},{6,7},{7,6},{8,9},{9,8},{10,11... | collective-permute-start | bytes 4423688 | tf_op jit(solution)/shard_map/ppermute | solution.py:429
  53.5 27.1 %collective-permute-start.11 = (bf16[8,96,768]{2,1,0:T(8,128)(2,1)}, bf16[8,96,768]{2,1,0:T(8,128)(2,1)}, u32[]{:S(2)}, u32[]{:S(2)}) collective-permute-start(bf16[8,96,768]{2,1,0:T(8,128)(2,1)} %bitcast.40), channel_id=1, source_target_pairs={{0,2},{2,0},{1,3},{3,1},{4,6},{6,4},{5,7},{7,5},{8,10},{10,8},{9,1... | collective-permute-start | bytes 3538952 | tf_op jit(solution)/shard_map/ppermute | solution.py:429
  56.1 6.4 %collective-permute-start.8 = (bf16[96,768]{1,0:T(8,128)(2,1)S(1)}, bf16[96,768]{1,0:T(8,128)(2,1)S(1)}, u32[]{:S(2)}, u32[]{:S(2)}) collective-permute-start(bf16[96,768]{1,0:T(8,128)(2,1)S(1)} %slice.69), channel_id=1, source_target_pairs={{0,32},{32,64},{64,96},{96,128},{128,160},{160,192},{192,224},{224... | collective-permute-start | bytes 442376 | tf_op jit(solution)/shard_map/ppermute | solution.py:449
  56.2 6.3 %collective-permute-start.9 = (bf16[96,768]{1,0:T(8,128)(2,1)S(1)}, bf16[96,768]{1,0:T(8,128)(2,1)S(1)}, u32[]{:S(2)}, u32[]{:S(2)}) collective-permute-start(bf16[96,768]{1,0:T(8,128)(2,1)S(1)} %slice.70), channel_id=1, source_target_pairs={{0,224},{32,0},{64,32},{96,64},{128,96},{160,128},{192,160},{224,1... | collective-permute-start | bytes 442376 | tf_op jit(solution)/shard_map/ppermute | solution.py:450
  63.7 16.9 %collective-permute-start.10 = (bf16[3,192,768]{2,1,0:T(8,128)(2,1)S(1)}, bf16[3,192,768]{2,1,0:T(8,128)(2,1)S(1)}, u32[]{:S(2)}, u32[]{:S(2)}) collective-permute-start(bf16[3,192,768]{2,1,0:T(8,128)(2,1)S(1)} %pad_maximum_fusion.1.far_ref.refs_6_), channel_id=1, source_target_pairs={{0,1},{1,0},{2,3},{3,2},{4,5},{5,4},{6,7},{7,6},{8,9},{9,8},{10,11... | collective-permute-start | bytes 2654216 | tf_op jit(solution)/shard_map/ppermute | solution.py:429
  63.8 53.6 %collective-permute-start.12 = (bf16[8,96,768]{2,1,0:T(8,128)(2,1)S(1)}, bf16[8,96,768]{2,1,0:T(8,128)(2,1)}, u32[]{:S(2)}, u32[]{:S(2)}) collective-permute-start(bf16[8,96,768]{2,1,0:T(8,128)(2,1)S(1)} %bitcast.43), channel_id=1, source_target_pairs={{0,1},{1,0},{2,3},{3,2},{4,5},{5,4},{6,7},{7,6},{8,9},{9,8},{10,11... | collective-permute-start | bytes 3538952 | tf_op jit(solution)/shard_map/ppermute | solution.py:429
  80.6 40.0 %collective-permute-start.13 = (bf16[8,96,768]{2,1,0:T(8,128)(2,1)}, bf16[8,96,768]{2,1,0:T(8,128)(2,1)}, u32[]{:S(2)}, u32[]{:S(2)}) collective-permute-start(bf16[8,96,768]{2,1,0:T(8,128)(2,1)} %collective-permute-done.11.by_ref.refs_9_), channel_id=1, source_target_pairs={{0,1},{1,0},{2,3},{3,2},{4,5},{5,4},{6,7},{7,6},{8,9},{9,8},{10,11... | collective-permute-start | bytes 3538952 | tf_op jit(solution)/shard_map/ppermute | solution.py:429
  88.7 8.0 %collective-permute-start.15 = (bf16[256,384]{1,0:T(8,128)(2,1)}, bf16[256,384]{1,0:T(8,128)(2,1)S(1)}, u32[]{:S(2)}, u32[]{:S(2)}) collective-permute-start(bf16[256,384]{1,0:T(8,128)(2,1)} %get-tuple-element.45.refs_3_), channel_id=1, source_target_pairs={{0,224},{32,0},{64,32},{96,64},{128,96},{160,128},{192,160},{224,1... | collective-permute-start | bytes 589832 | tf_op jit(solution)/shard_map/ppermute | solution.py:444
  89.0 8.5 %collective-permute-start.14 = (bf16[256,384]{1,0:T(8,128)(2,1)}, bf16[256,384]{1,0:T(8,128)(2,1)S(1)}, u32[]{:S(2)}, u32[]{:S(2)}) collective-permute-start(bf16[256,384]{1,0:T(8,128)(2,1)} %get-tuple-element.45.refs_3_), channel_id=1, source_target_pairs={{0,32},{32,64},{64,96},{96,128},{128,160},{160,192},{192,224},{224... | collective-permute-start | bytes 589832 | tf_op jit(solution)/shard_map/ppermute | solution.py:443
  90.7 10.2 %collective-permute-start.22 = (bf16[256,384]{1,0:T(8,128)(2,1)}, bf16[256,384]{1,0:T(8,128)(2,1)S(1)}, u32[]{:S(2)}, u32[]{:S(2)}) collective-permute-start(bf16[256,384]{1,0:T(8,128)(2,1)} %get-tuple-element.46.refs_11_), channel_id=1, source_target_pairs={{0,224},{32,0},{64,32},{96,64},{128,96},{160,128},{192,160},{224,1... | collective-permute-start | bytes 589832 | tf_op jit(solution)/shard_map/ppermute | solution.py:444
  96.7 7.6 %collective-permute-start.21 = (bf16[256,384]{1,0:T(8,128)(2,1)}, bf16[256,384]{1,0:T(8,128)(2,1)S(1)}, u32[]{:S(2)}, u32[]{:S(2)}) collective-permute-start(bf16[256,384]{1,0:T(8,128)(2,1)} %get-tuple-element.46.refs_11_), channel_id=1, source_target_pairs={{0,32},{32,64},{64,96},{96,128},{128,160},{160,192},{192,224},{224... | collective-permute-start | bytes 589832 | tf_op jit(solution)/shard_map/ppermute | solution.py:443
  97.5 7.2 %collective-permute-start.17 = (bf16[256,384]{1,0:T(8,128)(2,1)S(1)}, bf16[256,384]{1,0:T(8,128)(2,1)S(1)}, u32[]{:S(2)}, u32[]{:S(2)}) collective-permute-start(bf16[256,384]{1,0:T(8,128)(2,1)S(1)} %collective-permute-done.15.refs_5_), channel_id=1, source_target_pairs={{0,224},{32,0},{64,32},{96,64},{128,96},{160,128},{192,160},{224,1... | collective-permute-start | bytes 589832 | tf_op jit(solution)/shard_map/ppermute | solution.py:444
  100.9 7.8 %collective-permute-start.16 = (bf16[256,384]{1,0:T(8,128)(2,1)S(1)}, bf16[256,384]{1,0:T(8,128)(2,1)S(1)}, u32[]{:S(2)}, u32[]{:S(2)}) collective-permute-start(bf16[256,384]{1,0:T(8,128)(2,1)S(1)} %collective-permute-done.14.refs_4_), channel_id=1, source_target_pairs={{0,32},{32,64},{64,96},{96,128},{128,160},{160,192},{192,224},{224... | collective-permute-start | bytes 589832 | tf_op jit(solution)/shard_map/ppermute | solution.py:443
  104.3 5.8 %collective-permute-start.24 = (bf16[256,384]{1,0:T(8,128)(2,1)S(1)}, bf16[256,384]{1,0:T(8,128)(2,1)S(1)}, u32[]{:S(2)}, u32[]{:S(2)}) collective-permute-start(bf16[256,384]{1,0:T(8,128)(2,1)S(1)} %collective-permute-done.22.refs_13_), channel_id=1, source_target_pairs={{0,224},{32,0},{64,32},{96,64},{128,96},{160,128},{192,160},{224,1... | collective-permute-start | bytes 589832 | tf_op jit(solution)/shard_map/ppermute | solution.py:444
  104.7 9.0 %collective-permute-start.23 = (bf16[256,384]{1,0:T(8,128)(2,1)S(1)}, bf16[256,384]{1,0:T(8,128)(2,1)S(1)}, u32[]{:S(2)}, u32[]{:S(2)}) collective-permute-start(bf16[256,384]{1,0:T(8,128)(2,1)S(1)} %collective-permute-done.21.refs_12_), channel_id=1, source_target_pairs={{0,32},{32,64},{64,96},{96,128},{128,160},{160,192},{192,224},{224... | collective-permute-start | bytes 589832 | tf_op jit(solution)/shard_map/ppermute | solution.py:443
  108.7 8.0 %collective-permute-start.18 = (bf16[256,384]{1,0:T(8,128)(2,1)S(1)}, bf16[256,384]{1,0:T(8,128)(2,1)S(1)}, u32[]{:S(2)}, u32[]{:S(2)}) collective-permute-start(bf16[256,384]{1,0:T(8,128)(2,1)S(1)} %collective-permute-done.16.refs_6_), channel_id=1, source_target_pairs={{0,32},{32,64},{64,96},{96,128},{128,160},{160,192},{192,224},{224... | collective-permute-start | bytes 589832 | tf_op jit(solution)/shard_map/ppermute | solution.py:443
  110.1 7.3 %collective-permute-start.26 = (bf16[256,384]{1,0:T(8,128)(2,1)S(1)}, bf16[256,384]{1,0:T(8,128)(2,1)S(1)}, u32[]{:S(2)}, u32[]{:S(2)}) collective-permute-start(bf16[256,384]{1,0:T(8,128)(2,1)S(1)} %collective-permute-done.24.refs_15_), channel_id=1, source_target_pairs={{0,224},{32,0},{64,32},{96,64},{128,96},{160,128},{192,160},{224,1... | collective-permute-start | bytes 589832 | tf_op jit(solution)/shard_map/ppermute | solution.py:444
  113.6 15.0 %collective-permute-start.19 = (bf16[256,384]{1,0:T(8,128)(2,1)S(1)}, bf16[256,384]{1,0:T(8,128)(2,1)S(1)}, u32[]{:S(2)}, u32[]{:S(2)}) collective-permute-start(bf16[256,384]{1,0:T(8,128)(2,1)S(1)} %collective-permute-done.17.refs_7_), channel_id=1, source_target_pairs={{0,224},{32,0},{64,32},{96,64},{128,96},{160,128},{192,160},{224,1... | collective-permute-start | bytes 589832 | tf_op jit(solution)/shard_map/ppermute | solution.py:444
  116.7 11.9 %collective-permute-start.25 = (bf16[256,384]{1,0:T(8,128)(2,1)S(1)}, bf16[256,384]{1,0:T(8,128)(2,1)S(1)}, u32[]{:S(2)}, u32[]{:S(2)}) collective-permute-start(bf16[256,384]{1,0:T(8,128)(2,1)S(1)} %collective-permute-done.23.refs_14_), channel_id=1, source_target_pairs={{0,32},{32,64},{64,96},{96,128},{128,160},{160,192},{192,224},{224... | collective-permute-start | bytes 589832 | tf_op jit(solution)/shard_map/ppermute | solution.py:443
  117.4 11.3 %collective-permute-start.20 = (bf16[256,384]{1,0:T(8,128)(2,1)S(1)}, bf16[256,384]{1,0:T(8,128)(2,1)}, u32[]{:S(2)}, u32[]{:S(2)}) collective-permute-start(bf16[256,384]{1,0:T(8,128)(2,1)S(1)} %collective-permute-done.18.refs_8_), channel_id=1, source_target_pairs={{0,32},{32,64},{64,96},{96,128},{128,160},{160,192},{192,224},{224... | collective-permute-start | bytes 589832 | tf_op jit(solution)/shard_map/ppermute | solution.py:452
  117.4 11.3 %collective-permute-start.27 = (bf16[256,384]{1,0:T(8,128)(2,1)S(1)}, bf16[256,384]{1,0:T(8,128)(2,1)S(1)}, u32[]{:S(2)}, u32[]{:S(2)}) collective-permute-start(bf16[256,384]{1,0:T(8,128)(2,1)S(1)} %collective-permute-done.26.refs_17_), channel_id=1, source_target_pairs={{0,224},{32,0},{64,32},{96,64},{128,96},{160,128},{192,160},{224,1... | collective-permute-start | bytes 589832 | tf_op jit(solution)/shard_map/ppermute | solution.py:452
  141.2 112.8 %reduce-scatter.5.cloned.1.call-start = ((), (), s32[]{:S(2)}) async-start(), calls=%async_computation.4 | async-start | bytes 3981312 | tf_op jit(solution)/shard_map/reduce_scatter | solution.py:509
  156.9 28.2 %collective-permute-start.29 = (bf16[8,96,768]{2,1,0:T(8,128)(2,1)}, bf16[8,96,768]{2,1,0:T(8,128)(2,1)S(1)}, u32[]{:S(2)}, u32[]{:S(2)}) collective-permute-start(bf16[8,96,768]{2,1,0:T(8,128)(2,1)} %get-tuple-element.50), channel_id=1, source_target_pairs={{0,2},{2,0},{1,3},{3,1},{4,6},{6,4},{5,7},{7,5},{8,10},{10,8},{9,1... | collective-permute-start | bytes 3538952 | tf_op jit(solution)/shard_map/ppermute | solution.py:429
  220.3 31.5 %all-to-all-start = ((bf16[8,272,384]{2,1,0:T(8,128)(2,1)}), bf16[8,272,384]{2,1,0:T(8,128)(2,1)S(1)}, u32[]{:S(2)}, u32[]{:S(2)}) async-start(bf16[8,272,384]{2,1,0:T(8,128)(2,1)} %pad_maximum_fusion), calls=%async_computation.2 | async-start | bytes 3342336 | tf_op jit(solution)/shard_map/all_to_all | solution.py:521
  (27 other events, 331.6 us)
Sparse Core Ops, SparseCore 0:
  10.3 43.1 all-gather.2
  141.3 45.7 reduce-scatter.2
  204.6 48.4 reduce-scatter.4
where the time goes:
time: 269 us
  waiting for transfers between devices  121 us (45%)
  Pallas kernels  68.1 us (25%)
  starting transfers between devices  43.3 us (16%)
  between operations  14.1 us (5%)
  other arithmetic  13 us (5%)
  local copies, waits for them, and re-layouts  8.51 us (3%)
    ppermute x10, waiting for transfers between devices, swap(): return lax.ppermute(value, axis, [(0, 1), (1, 0)])  60.2 us
    all_to_all x1, waiting for transfers between devices, layer(): load = lax.all_to_all(load, ('x', 'yhi'), 0, 0, tiled=True)  24 us
    ppermute x9, waiting for transfers between devices, ring_gather(): high = lax.ppermute(high, 'seq', up)  23.2 us
    pallas_call x4, Pallas kernels, call(): pl.pallas_call(body, in_specs=[VMEM] * len(operands), out_shape=[jax.Shap...  20.7 us
    ppermute x9, starting transfers between devices, ring_gather(): low = lax.ppermute(low, 'seq', down)  19.9 us
    pallas_call x1, Pallas kernels, attend(): pl.pallas_call(lambda *refs: attend_body(*refs, count=len(sizes)), grid_s...  11.7 us
    pallas_call x1, Pallas kernels, inner(): pl.pallas_call(lambda *refs: inner_body(*refs, close=close), grid_spec=pl...  10.9 us
    pallas_call x1, Pallas kernels, prepare(): pl.pallas_call(prepare_body, grid_spec=pltpu.PrefetchScalarGridSpec(num_s...  9.92 us
  transfers between devices with their start and end apart: 36, of which 22 were waited for; matrix products, arithmetic and copies ran while one was open for 4% of the time, Pallas kernels for 17%

commit v1 on v0

--- a/solution.py
+++ b/solution.py
@@ -28,123 +28,111 @@
     return (gradient - mean_grad - normed * mean_both) * inverse
 
 
+VMEM = pl.BlockSpec(memory_space=pltpu.VMEM)
+SMEM = pl.BlockSpec(memory_space=pltpu.SMEM)
 ARBITRARY = pltpu.CompilerParams(dimension_semantics=("arbitrary",))
 
 
-def prepare_body(
-    me_ref, tok_ref, cot_ref, unit_ref, inv_ref, xk_ref, xs_ref, xr_ref, ck_ref, cs_ref, cr_ref, mean_ref
-):
-    step = pl.program_id(0)
-    rows = tok_ref.shape[0]
-    group, _, own, _ = xk_ref.shape
-    block = 4 * own
-    core = me_ref[1]
-
-    @pl.when(step == 0)
+def arrange(me_ref, value, s, keep_ref, send_ref, plain_ref):
+    own, rows = keep_ref.shape[2:]
+    turned = value.T
+
+    def place(c):
+        for y in range(2):
+            away_y = lax.rem(me_ref[2] + y, 2)
+            for ref, at in ((keep_ref, 2 * y + c), (send_ref, 2 * y + 1 - c)):
+                ref[s, away_y] = turned[at * own : (at + 1) * own]
+
+    @pl.when(me_ref[1] == 0)
     def _():
-        values = tok_ref[...].astype(F32)
-        average = jnp.mean(values, axis=-1, keepdims=True)
-        centered = values - average
-        inverse = lax.rsqrt(jnp.mean(centered * centered, axis=-1, keepdims=True) + epsilon)
-        mean_ref[...] = jnp.broadcast_to(average, (rows, HD))
-        inv_ref[...] = jnp.broadcast_to(inverse, (rows, HD))
+        place(0)
+
+    @pl.when(me_ref[1] == 1)
+    def _():
+        place(1)
+
+    for c, ref in enumerate((keep_ref, send_ref)):
+        plain_ref[s, c] = ref[s].reshape(2 * own, rows).T
+
+
+def tokens_body(me_ref, tok_ref, unit_ref, inv_ref, keep_ref, send_ref, plain_ref, mean_ref):
+    rows, features = tok_ref.shape
+    slabs = keep_ref.shape[0]
+    block = features // slabs
+    values = tok_ref[...].astype(F32)
+    average = jnp.mean(values, axis=-1, keepdims=True)
+    centered = values - average
+    inverse = lax.rsqrt(jnp.mean(centered * centered, axis=-1, keepdims=True) + epsilon)
+    mean_ref[...] = jnp.broadcast_to(average, (rows, HD))
+    inv_ref[...] = jnp.broadcast_to(inverse, (rows, HD))
 
     def slab(s, carry):
-        here = pl.ds(pl.multiple_of((step * group + s) * block, HD), block)
-        there = pl.ds(pl.multiple_of(s * block, HD), block)
+        here = pl.ds(pl.multiple_of(s * block, HD), block)
         unit = (tok_ref[:, here].astype(F32) - mean_ref[:, :1]) * inv_ref[:, :1]
-        unit_ref[:, there] = unit
-        for value, refs in (
-            (unit.astype(BF), (xk_ref, xs_ref, xr_ref)),
-            (cot_ref[:, here], (ck_ref, cs_ref, cr_ref)),
-        ):
-            turned = value.T
-
-            def place(refs, turned, c):
-                for y in range(2):
-                    away_y = lax.rem(me_ref[2] + y, 2)
-                    at = (2 * y + c) * own
-                    refs[0][s, away_y] = turned[at : at + own]
-                    at = (2 * y + 1 - c) * own
-                    refs[1][s, away_y] = turned[at : at + own]
-
-            @pl.when(core == 0)
-            def _():
-                place(refs, turned, 0)
-
-            @pl.when(core == 1)
-            def _():
-                place(refs, turned, 1)
-
-            for c in range(2):
-                refs[2][s, c] = refs[c][s].reshape(2 * own, rows).T
+        unit_ref[:, here] = unit
+        arrange(me_ref, unit.astype(BF), s, keep_ref, send_ref, plain_ref)
         return carry
 
-    lax.fori_loop(0, group, slab, 0)
-
-
-def prepare(me, tokens, cotangent, slabs, steps=4):
-    rows, features = tokens.shape
+    lax.fori_loop(0, slabs, slab, 0)
+
+
+def cotangent_body(me_ref, cot_ref, keep_ref, send_ref, plain_ref):
+    slabs = keep_ref.shape[0]
+    block = cot_ref.shape[1] // slabs
+
+    def slab(s, carry):
+        here = pl.ds(pl.multiple_of(s * block, HD), block)
+        arrange(me_ref, cot_ref[:, here], s, keep_ref, send_ref, plain_ref)
+        return carry
+
+    lax.fori_loop(0, slabs, slab, 0)
+
+
+def prepare(me, values, slabs, tokens):
+    rows, features = values.shape
     own = features // slabs // 4
-    group = slabs // steps
-    whole = pl.BlockSpec((rows, features), lambda i, me: (0, 0))
-    turned = pl.BlockSpec((group, 2, own, rows), lambda i, me: (i, 0, 0, 0))
-    plain = pl.BlockSpec((group, 2, rows, 2 * own), lambda i, me: (i, 0, 0, 0))
-    turned_shape = jax.ShapeDtypeStruct((slabs, 2, own, rows), BF)
-    plain_shape = jax.ShapeDtypeStruct((slabs, 2, rows, 2 * own), BF)
+    turned = jax.ShapeDtypeStruct((slabs, 2, own, rows), BF)
+    extra = [
+        jax.ShapeDtypeStruct((rows, features), F32),
+        jax.ShapeDtypeStruct((rows, HD), F32),
+    ]
     return pl.pallas_call(
-        prepare_body,
-        grid_spec=pltpu.PrefetchScalarGridSpec(
-            num_scalar_prefetch=1,
-            grid=(steps,),
-            in_specs=[whole, whole],
-            out_specs=[
-                pl.BlockSpec((rows, features // steps), lambda i, me: (0, i)),
-                pl.BlockSpec((rows, HD), lambda i, me: (0, 0)),
-            ]
-            + [turned, turned, plain] * 2,
-            scratch_shapes=[pltpu.VMEM((rows, HD), F32)],
-        ),
-        out_shape=[
-            jax.ShapeDtypeStruct((rows, features), F32),
-            jax.ShapeDtypeStruct((rows, HD), F32),
-        ]
-        + [turned_shape, turned_shape, plain_shape] * 2,
-        compiler_params=ARBITRARY,
-        name="prepare",
-    )(me, tokens, cotangent)
+        tokens_body if tokens else cotangent_body,
+        in_specs=[SMEM, VMEM],
+        out_shape=(extra if tokens else [])
+        + [turned, turned, jax.ShapeDtypeStruct((slabs, 2, rows, 2 * own), BF)],
+        scratch_shapes=[pltpu.VMEM((rows, HD), F32)] if tokens else [],
+        name="prepare_tokens" if tokens else "prepare_cotangent",
+    )(me, values)
 
 
 def distance(i):
     return (i + 1) // 2 * (1 if i % 2 == 0 else -1)
 
 
-def far_from(i):
-    return lax.div(i + 1, 2) * (1 - 2 * lax.rem(i, 2))
-
-
-def project_kv_body(
-    me_ref, x_ref, near_ref, near_far_ref, far_ref, far_far_ref, k_ref, kl_ref, vl_ref, acc_ref
-):
+def project_kv_body(me_ref, x_ref, near_ref, near_far_ref, far_ref, far_far_ref, k_ref, kv_ref):
     slabs = x_ref.shape[0]
-    width = k_ref.shape[1]
+    rows, width = k_ref.shape
     close = near_ref.shape[0]
-    acc_ref[...] = jnp.zeros_like(acc_ref)
-
-    def take(mine_ref, theirs_ref, first):
-        def step(k, carry):
-            slab = lax.rem(me_ref[0] + slabs + far_from(k + first), slabs)
-            acc_ref[...] += dot(x_ref[slab, 0], mine_ref[k]) + dot(x_ref[slab, 1], theirs_ref[k])
-            return carry
-
-        lax.fori_loop(0, mine_ref.shape[0], step, 0)
-
-    take(near_ref, near_far_ref, 0)
-    take(far_ref, far_far_ref, close)
-    k_ref[...] = acc_ref[:, :width]
-    for at in range(0, width, HD):
-        kl_ref[:, at : at + HD] = normalize(acc_ref[:, at : at + HD])[0].astype(BF)
-    vl_ref[...] = acc_ref[:, width:].astype(BF)
+    for n in range(2 * width // 256):
+        cols = slice(n * 256, (n + 1) * 256)
+        acc = jnp.zeros((rows, 256), F32)
+        for i in range(slabs):
+            slab = lax.rem(me_ref[0] + slabs + distance(i), slabs)
+            if i < close:
+                pieces = near_ref[i, :, cols], near_far_ref[i, :, cols]
+            else:
+                pieces = far_ref[i - close, :, cols], far_far_ref[i - close, :, cols]
+            for c, piece in enumerate(pieces):
+                acc = acc + dot(x_ref[slab, c], piece)
+        for j in range(2):
+            at = n * 256 + j * HD
+            part = acc[:, j * HD : (j + 1) * HD]
+            if at < width:
+                k_ref[:, at : at + HD] = part
+                kv_ref[:rows, at : at + HD] = normalize(part)[0].astype(BF)
+            else:
+                kv_ref[rows:, at - width : at - width + HD] = part.astype(BF)
 
 
 def project_kv(me, x, near, near_far, far, far_far):
@@ -154,36 +142,24 @@
         in_specs=[pl.BlockSpec(memory_space=pltpu.SMEM)] + [pl.BlockSpec(memory_space=pltpu.VMEM)] * 5,
         out_shape=[
             jax.ShapeDtypeStruct((rows, width), F32),
-            jax.ShapeDtypeStruct((rows, width), BF),
-            jax.ShapeDtypeStruct((rows, width), BF),
+            jax.ShapeDtypeStruct((2 * rows, width), BF),
         ],
-        scratch_shapes=[pltpu.VMEM((rows, 2 * width), F32)],
         name="project_kv",
     )(me, x, near, near_far, far, far_far)
 
 
-def project_qo_body(x_ref, c_ref, b_ref, by_ref, bc_ref, byc_ref, q_ref, g_ref, acc_ref):
+def project_qo_body(x_ref, c_ref, b_ref, by_ref, bc_ref, byc_ref, q_ref, g_ref):
     slabs = x_ref.shape[0]
-    width = q_ref.shape[1]
-    acc_ref[...] = jnp.zeros_like(acc_ref)
-
-    def step(k, carry):
-        for left_ref, at in ((x_ref, 0), (c_ref, width)):
-            cols = slice(at, at + width)
-            part = 0.0
-            for c, (first, second) in enumerate(((b_ref, by_ref), (bc_ref, byc_ref))):
-                piece = jnp.concatenate([first[k, :, cols], second[k, :, cols]], axis=0)
-                part = part + dot(left_ref[k, c], piece)
-            acc_ref[:, cols] += part
-        return carry
-
-    lax.fori_loop(0, slabs, step, 0)
-    q_ref[...] = acc_ref[:, :width]
-    g_ref[...] = acc_ref[:, width:].astype(BF)
-
-
-VMEM = pl.BlockSpec(memory_space=pltpu.VMEM)
-SMEM = pl.BlockSpec(memory_space=pltpu.SMEM)
+    rows, width = q_ref.shape
+    for left_ref, out_ref, first in ((x_ref, q_ref, 0), (c_ref, g_ref, width)):
+        for at, size in ((0, 256), (256, 128)):
+            cols = slice(first + at, first + at + size)
+            acc = jnp.zeros((rows, size), F32)
+            for k in range(slabs):
+                for c, (one, two) in enumerate(((b_ref, by_ref), (bc_ref, byc_ref))):
+                    piece = jnp.concatenate([one[k, :, cols], two[k, :, cols]], axis=0)
+                    acc = acc + dot(left_ref[k, c], piece)
+            out_ref[:, at : at + size] = acc.astype(out_ref.dtype)
 
 
 def project_qo(x, c, *pieces):
@@ -192,16 +168,17 @@
         project_qo_body,
         in_specs=[VMEM] * 6,
         out_shape=[jax.ShapeDtypeStruct((rows, width), F32), jax.ShapeDtypeStruct((rows, width), BF)],
-        scratch_shapes=[pltpu.VMEM((rows, 2 * width), F32)],
         name="project_qo",
     )(x, c, *pieces)
 
 
-def attend_body(me_ref, q_ref, g_ref, *refs, count):
-    k_refs, v_refs = refs[:count], refs[count : 2 * count]
-    att_ref, qb_ref, pair_ref, e_ref = refs[2 * count :]
+def attend_body(me_ref, q_ref, g_ref, *refs):
+    pieces = refs[:-4]
+    att_ref, qb_ref, pair_ref, e_ref = refs[-4:]
     slabs = pair_ref.shape[0]
     rows = q_ref.shape[0]
+    k_refs = [ref.at[:rows] for ref in pieces[:-2]] + [pieces[-2]]
+    v_refs = [ref.at[rows:] for ref in pieces[:-2]] + [pieces[-1]]
     scale = HD ** (-0.5)
     q_unit, q_inv = normalize(q_ref[...])
     q = q_unit.astype(BF)
@@ -236,24 +213,25 @@
     qb_ref[...] = normalize_back(dq_t.T, q_unit, q_inv).astype(BF)
 
 
-def attend(me, q, g, keys, values):
+def attend(me, q, g, pieces):
     rows, width = q.shape
-    sizes = [k.shape[0] for k in keys]
-    shape = (sum(sizes) // rows, 2, rows, width)
+    sizes = [v.shape[0] for v in pieces]
+    total = sum(sizes) // 2
+    shape = (total // rows, 2, rows, width)
     row_spec = pl.BlockSpec((rows, HD), lambda h, me: (0, h))
     specs = [pl.BlockSpec((n, HD), lambda h, me: (0, h)) for n in sizes]
     return pl.pallas_call(
-        lambda *refs: attend_body(*refs, count=len(sizes)),
+        attend_body,
         grid_spec=pltpu.PrefetchScalarGridSpec(
             num_scalar_prefetch=1,
             grid=(width // HD,),
-            in_specs=[row_spec, row_spec] + specs * 2,
+            in_specs=[row_spec, row_spec] + specs,
             out_specs=[
                 row_spec,
                 row_spec,
                 pl.BlockSpec((*shape[:3], HD), lambda h, me: (0, 0, 0, h)),
             ],
-            scratch_shapes=[pltpu.VMEM((sum(sizes), rows), F32)],
+            scratch_shapes=[pltpu.VMEM((total, rows), F32)],
         ),
         out_shape=[
             jax.ShapeDtypeStruct((rows, width), BF),
@@ -262,7 +240,7 @@
         ],
         compiler_params=ARBITRARY,
         name="attend",
-    )(me, q, g, *keys, *values)
+    )(me, q, g, *pieces)
 
 
 def terms_of(x_ref, c_ref, a_ref, b_ref, store):
@@ -434,7 +412,7 @@
     return [(i, (i + 1) % size) for i in range(size)], [(i, (i - 1) % size) for i in range(size)]
 
 
-def ring_gather(value, held=None, last=None):
+def ring_gather(value, held=None):
     up, down = turns()
     half = value.shape[0] // 2
     rows = [value]
@@ -445,11 +423,8 @@
         if step == 0 and held is not None:
             high, low, held = lax.optimization_barrier((high, low, held))
         rows += [high, low]
-    if last is None:
-        rows.append(lax.ppermute(high[:half], "seq", up))
-        rows.append(lax.ppermute(low[half:], "seq", down))
-    else:
-        rows.append(lax.ppermute(high, "seq", up) if last else lax.ppermute(low, "seq", down))
+    rows.append(lax.ppermute(high[:half], "seq", up))
+    rows.append(lax.ppermute(low[half:], "seq", down))
     return rows if held is None else (rows, held)
 
 
@@ -475,20 +450,21 @@
     kv_weight = qkv_weight[:, 1:].reshape(own, 2 * width)
     qo_weight = jnp.concatenate([qkv_weight[:, 0], out_weight], axis=1)
     qo_mine = lax.all_gather(qo_weight, "seq")
-    kv_weight = jnp.concatenate([kv_weight, swap(kv_weight, "ylo")], axis=0)
-    unit, inverse, *turned = prepare(me, tokens[0], cotangent[0], slabs)
-    x_keep, x_send, x_r, c_keep, c_send, c_r = turned
-    ring, x_r = ring_gather(kv_weight, x_r)
+    kv_y = swap(kv_weight, "ylo")
+    kv_weight = jnp.concatenate([kv_weight, kv_y], axis=0)
+    unit, inverse, x_keep, x_send, x_r = prepare(me, tokens[0], slabs, True)
+    c_keep, c_send, c_r = prepare(me, cotangent[0], slabs, False)
+    kv_weight, x_r = lax.optimization_barrier((kv_weight, x_r))
+    ring, c_r = ring_gather(kv_weight, c_r)
     ring = whole(ring)
     near, far = jnp.stack(ring[:5]), jnp.stack(ring[5:])
     near_far, far_far = swap(near, "core"), swap(far, "core")
     qo_y = swap(qo_mine, "ylo")
-    key, key_low, value_low = project_kv(me, x_r, near, near_far, far, far_far)
-    keys = ring_gather(key_low, last=True)
-    values = ring_gather(value_low, last=False)
+    key, key_value = project_kv(me, x_r, near, near_far, far, far_far)
+    every = ring_gather(key_value)
     qo_pieces = (qo_mine, qo_y, swap(qo_mine, "core"), swap(qo_y, "core"))
     query, grad_rows = project_qo(x_r, c_r, *qo_pieces)
-    attended, query_back, pair = attend(me, query, grad_rows, keys, values)
+    attended, query_back, pair = attend(me, query, grad_rows, every)
     pair = lax.psum_scatter(
         pair.reshape(slabs * 2 * row_count, width), "seq", scatter_dimension=0, tiled=True
     )

time: 269 us -> 271 us (level)
    ppermute x9 -> x6, waiting for transfers between devices: 7.45 us -> 20.2 us  [ring_gather(): low = lax.ppermute(low, 'seq', down)]
    ppermute x10, waiting for transfers between devices: 60.2 us -> 51.8 us  [swap(): return lax.ppermute(value, axis, [(0, 1), (1, 0)])]
    ppermute x9 -> x6, waiting for transfers between devices: 23.2 us -> 18.5 us  [ring_gather(): high = lax.ppermute(high, 'seq', up)]
    ppermute x1 -> x2, starting transfers between devices: 3.28 us -> 6.98 us  [ring_gather(): rows.append(lax.ppermute(low[half:], 'seq', down))]
    ppermute x9 -> x6, starting transfers between devices: 3.37 us -> 0.09 us  [ring_gather(): high = lax.ppermute(high, 'seq', up)]
    ppermute x2 -> x0, starting transfers between devices: 3.23 us -> none  [the longest x1 3.23 us: ring_gather(): lax.ppermute(low, 'seq', down)]
    pallas_call x2 -> x3, Pallas kernels: 21.6 us -> 24.6 us  [the longest x2 12.9 us: prepare(): pl.pallas_call(tokens_body if tokens else cotangent_body, in_specs=[SMEM,...]
    ppermute x9 -> x6, starting transfers between devices: 19.9 us -> 22.5 us  [ring_gather(): low = lax.ppermute(low, 'seq', down)]
  transfers between devices with their start and end apart: 36 -> 30, of which waited for: 22 -> 15; matrix products, arithmetic and copies ran while one was open for 4% -> 4% of each run, Pallas kernels for 17% -> 17%
where the time goes in v1:
time: 271 us; the launch traced here: 270 us
  waiting for transfers between devices  121 us (45%)
  Pallas kernels  68.6 us (25%)
  starting transfers between devices  43.8 us (16%)
  between operations  14 us (5%)
  other arithmetic  12 us (4%)
  local copies, waits for them, and re-layouts  10.4 us (4%)
    ppermute x10, waiting for transfers between devices, swap(): return lax.ppermute(value, axis, [(0, 1), (1, 0)])  51.8 us
    all_to_all x1, waiting for transfers between devices, layer(): load = lax.all_to_all(load, ('x', 'yhi'), 0, 0, tiled=True)  24 us
    ppermute x6, starting transfers between devices, ring_gather(): low = lax.ppermute(low, 'seq', down)  22.5 us
    pallas_call x4, Pallas kernels, call(): pl.pallas_call(body, in_specs=[VMEM] * len(operands), out_shape=[jax.Shap...  20.9 us
    ppermute x6, waiting for transfers between devices, ring_gather(): low = lax.ppermute(low, 'seq', down)  20.2 us
    ppermute x6, waiting for transfers between devices, ring_gather(): high = lax.ppermute(high, 'seq', up)  18.5 us
    pallas_call x2, Pallas kernels, prepare(): pl.pallas_call(tokens_body if tokens else cotangent_body, in_specs=[SMEM,...  12.9 us
    pallas_call x1, Pallas kernels, attend(): pl.pallas_call(attend_body, grid_spec=pltpu.PrefetchScalarGridSpec(num_sc...  11.7 us
  transfers between devices with their start and end apart: 30, of which 15 were waited for; matrix products, arithmetic and copies ran while one was open for 4% of the time, Pallas kernels for 17%

profile of v1, /device:TPU:16, one launch (start us, length us, event | category | flops | bytes accessed | tf_op | source)
XLA Modules:
  0.0 270.0 jit_solution(13867845541816258272)
XLA Ops:
  12.7 7.8 %prepare_tokens.1 = (f32[256,3072]{1,0:T(8,128)}, f32[256,128]{1,0:T(8,128)}, bf16[8,2,96,256]{3,2,1,0:T(8,128)(2,1)}, bf16[8,2,96,256]{3,2,1,0:T(8,128)(2,1)}, bf16[8,2,256,192]{3,2,1,0:T(8,128)(2,1)}) custom-call(s32[3]{0:T(128)} %pad_add_fusion.me_ref.refs_0_, bf16[256,3072]{1,0:T(8,128)(2,1)} %bitcast.45), custom_call_target="tpu_custom_call" | custom-call | tf_op jit(solution)/shard_map/prepare_tokens/pallas_call | solution.py:99
  20.5 5.9 %collective-permute-start.2 = (bf16[192,768]{1,0:T(8,128)(2,1)S(1)}, bf16[192,768]{1,0:T(8,128)(2,1)S(1)}, u32[]{:S(2)}, u32[]{:S(2)}) collective-permute-start(bf16[192,768]{1,0:T(8,128)(2,1)S(1)} %pad_maximum_fusion.3), channel_id=1, source_target_pairs={{0,224},{32,0},{64,32},{96,64},{128,96},{160,128},{192,160},{224,1... | collective-permute-start | bytes 884744 | tf_op jit(solution)/shard_map/ppermute | solution.py:422
  26.4 5.1 %prepare_cotangent.1 = (bf16[8,2,96,256]{3,2,1,0:T(8,128)(2,1)}, bf16[8,2,96,256]{3,2,1,0:T(8,128)(2,1)}, bf16[8,2,256,192]{3,2,1,0:T(8,128)(2,1)}) custom-call(s32[3]{0:T(128)} %pad_add_fusion.me_ref.refs_0_, bf16[256,3072]{1,0:T(8,128)(2,1)} %bitcast.46), custom_call_target="tpu_custom_call" | custom-call | tf_op jit(solution)/shard_map/prepare_cotangent/pallas_call | solution.py:99
  31.6 3.2 %collective-permute-done.2 = bf16[192,768]{1,0:T(8,128)(2,1)S(1)} collective-permute-done((bf16[192,768]{1,0:T(8,128)(2,1)S(1)}, bf16[192,768]{1,0:T(8,128)(2,1)S(1)}, u32[]{:S(2)}, u32[]{:S(2)}) %collective-permute-start.2) | collective-permute-done | bytes 294944 | tf_op jit(solution)/shard_map/ppermute | solution.py:422
  34.8 4.9 %collective-permute-done.1 = bf16[192,768]{1,0:T(8,128)(2,1)S(1)} collective-permute-done((bf16[192,768]{1,0:T(8,128)(2,1)S(1)}, bf16[192,768]{1,0:T(8,128)(2,1)S(1)}, u32[]{:S(2)}, u32[]{:S(2)}) %collective-permute-start.1) | collective-permute-done | bytes 294944 | tf_op jit(solution)/shard_map/ppermute | solution.py:421
  39.6 3.2 %collective-permute-start.4 = (bf16[192,768]{1,0:T(8,128)(2,1)S(1)}, bf16[192,768]{1,0:T(8,128)(2,1)S(1)}, u32[]{:S(2)}, u32[]{:S(2)}) collective-permute-start(bf16[192,768]{1,0:T(8,128)(2,1)S(1)} %collective-permute-done.2), channel_id=1, source_target_pairs={{0,224},{32,0},{64,32},{96,64},{128,96},{160,128},{192,160},{224,1... | collective-permute-start | bytes 884744 | tf_op jit(solution)/shard_map/ppermute | solution.py:422
  42.9 9.1 %collective-permute-done.3 = bf16[192,768]{1,0:T(8,128)(2,1)S(1)} collective-permute-done((bf16[192,768]{1,0:T(8,128)(2,1)S(1)}, bf16[192,768]{1,0:T(8,128)(2,1)S(1)}, u32[]{:S(2)}, u32[]{:S(2)}) %collective-permute-start.3) | collective-permute-done | bytes 294944 | tf_op jit(solution)/shard_map/ppermute | solution.py:421
  52.0 3.2 %collective-permute-start.7 = (bf16[192,768]{1,0:T(8,128)(2,1)S(1)}, bf16[192,768]{1,0:T(8,128)(2,1)S(1)}, u32[]{:S(2)}, u32[]{:S(2)}) collective-permute-start(bf16[192,768]{1,0:T(8,128)(2,1)S(1)} %collective-permute-done.4), channel_id=1, source_target_pairs={{0,224},{32,0},{64,32},{96,64},{128,96},{160,128},{192,160},{224,1... | collective-permute-start | bytes 884744 | tf_op jit(solution)/shard_map/ppermute | solution.py:422
  55.4 4.5 %collective-permute-done.6 = bf16[192,768]{1,0:T(8,128)(2,1)S(1)} collective-permute-done((bf16[192,768]{1,0:T(8,128)(2,1)S(1)}, bf16[192,768]{1,0:T(8,128)(2,1)S(1)}, u32[]{:S(2)}, u32[]{:S(2)}) %collective-permute-start.6) | collective-permute-done | bytes 294944 | tf_op jit(solution)/shard_map/ppermute | solution.py:421
  60.1 3.3 %collective-permute-start.9 = (bf16[96,768]{1,0:T(8,128)(2,1)S(1)}, bf16[96,768]{1,0:T(8,128)(2,1)S(1)}, u32[]{:S(2)}, u32[]{:S(2)}) collective-permute-start(bf16[96,768]{1,0:T(8,128)(2,1)S(1)} %slice.78), channel_id=1, source_target_pairs={{0,224},{32,0},{64,32},{96,64},{128,96},{160,128},{192,160},{224,1... | collective-permute-start | bytes 442376 | tf_op jit(solution)/shard_map/ppermute | solution.py:427
  72.1 5.6 %project_kv.1 = (f32[256,384]{1,0:T(8,128)}, bf16[512,384]{1,0:T(8,128)(2,1)}) custom-call(s32[3]{0:T(128)} %pad_add_fusion.me_ref.refs_0_, bf16[8,2,256,192]{3,2,1,0:T(8,128)(2,1)} %get-tuple-element.38.x_ref, bf16[5,192,768]{2,1,0:T(8,128)(2,1)} %copy-done.1, bf16[5,192,768]{2,1,0:T(8,128)(2,1)} %collective-permute-done.5.near_far_ref.refs_5_, ...), custom_call_target="tpu_custom_call" | custom-call | tf_op jit(solution)/shard_map/project_kv/pallas_call | solution.py:140
  77.7 3.3 %collective-permute-start.15 = (bf16[512,384]{1,0:T(8,128)(2,1)}, bf16[512,384]{1,0:T(8,128)(2,1)S(1)}, u32[]{:S(2)}, u32[]{:S(2)}) collective-permute-start(bf16[512,384]{1,0:T(8,128)(2,1)} %get-tuple-element.48.refs_0_), channel_id=1, source_target_pairs={{0,224},{32,0},{64,32},{96,64},{128,96},{160,128},{192,160},{224,1... | collective-permute-start | bytes 1179656 | tf_op jit(solution)/shard_map/ppermute | solution.py:422
  81.0 10.3 %collective-permute-done.11.by_ref.refs_9_ = bf16[8,96,768]{2,1,0:T(8,128)(2,1)} collective-permute-done((bf16[8,96,768]{2,1,0:T(8,128)(2,1)}, bf16[8,96,768]{2,1,0:T(8,128)(2,1)}, u32[]{:S(2)}, u32[]{:S(2)}) %collective-permute-start.11) | collective-permute-done | bytes 1179680 | tf_op jit(solution)/shard_map/ppermute | solution.py:407
  91.3 3.1 %collective-permute-start.17 = (bf16[512,384]{1,0:T(8,128)(2,1)S(1)}, bf16[512,384]{1,0:T(8,128)(2,1)S(1)}, u32[]{:S(2)}, u32[]{:S(2)}) collective-permute-start(bf16[512,384]{1,0:T(8,128)(2,1)S(1)} %collective-permute-done.15.refs_2_), channel_id=1, source_target_pairs={{0,224},{32,0},{64,32},{96,64},{128,96},{160,128},{192,160},{224,1... | collective-permute-start | bytes 1179656 | tf_op jit(solution)/shard_map/ppermute | solution.py:422
  94.5 9.0 %collective-permute-done.17.refs_4_ = bf16[512,384]{1,0:T(8,128)(2,1)S(1)} collective-permute-done((bf16[512,384]{1,0:T(8,128)(2,1)S(1)}, bf16[512,384]{1,0:T(8,128)(2,1)S(1)}, u32[]{:S(2)}, u32[]{:S(2)}) %collective-permute-start.17) | collective-permute-done | bytes 393248 | tf_op jit(solution)/shard_map/ppermute | solution.py:422
  103.4 3.7 %collective-permute-start.19 = (bf16[512,384]{1,0:T(8,128)(2,1)S(1)}, bf16[512,384]{1,0:T(8,128)(2,1)S(1)}, u32[]{:S(2)}, u32[]{:S(2)}) collective-permute-start(bf16[512,384]{1,0:T(8,128)(2,1)S(1)} %collective-permute-done.17.refs_4_), channel_id=1, source_target_pairs={{0,224},{32,0},{64,32},{96,64},{128,96},{160,128},{192,160},{224,1... | collective-permute-start | bytes 1179656 | tf_op jit(solution)/shard_map/ppermute | solution.py:422
  107.2 8.0 %collective-permute-done.19.refs_6_ = bf16[512,384]{1,0:T(8,128)(2,1)S(1)} collective-permute-done((bf16[512,384]{1,0:T(8,128)(2,1)S(1)}, bf16[512,384]{1,0:T(8,128)(2,1)S(1)}, u32[]{:S(2)}, u32[]{:S(2)}) %collective-permute-start.19) | collective-permute-done | bytes 393248 | tf_op jit(solution)/shard_map/ppermute | solution.py:422
  116.0 3.7 %collective-permute-start.21 = (bf16[256,384]{1,0:T(8,128)(2,1)}, bf16[256,384]{1,0:T(8,128)(2,1)}, u32[]{:S(2)}, u32[]{:S(2)}) collective-permute-start(bf16[256,384]{1,0:T(8,128)(2,1)} %slice.80), channel_id=1, source_target_pairs={{0,224},{32,0},{64,32},{96,64},{128,96},{160,128},{192,160},{224,1... | collective-permute-start | bytes 589832 | tf_op jit(solution)/shard_map/ppermute | solution.py:427
  122.6 6.5 %project_qo.1 = (f32[256,384]{1,0:T(8,128)}, bf16[256,384]{1,0:T(8,128)(2,1)}) custom-call(bf16[8,2,256,192]{3,2,1,0:T(8,128)(2,1)} %get-tuple-element.38.x_ref, bf16[8,2,256,192]{3,2,1,0:T(8,128)(2,1)} %get-tuple-element.45.c_ref, bf16[8,96,768]{2,1,0:T(8,128)(2,1)} %bitcast.41, bf16[8,96,768]{2,1,0:T(8,128)(2,1)} %collective-permute-done.11.by_ref.refs_9_, ...), custom_call_target="tpu_custom_call" | custom-call | tf_op jit(solution)/shard_map/project_qo/pallas_call | solution.py:167
  129.2 11.7 %attend.1 = (bf16[256,384]{1,0:T(8,128)(2,1)}, bf16[256,384]{1,0:T(8,128)(2,1)}, bf16[8,2,256,384]{3,2,1,0:T(8,128)(2,1)}) custom-call(s32[3]{0:T(128)} %pad_add_fusion.me_ref.refs_0_, f32[256,384]{1,0:T(8,128)} %get-tuple-element.46.q_ref, bf16[256,384]{1,0:T(8,128)(2,1)} %get-tuple-element.47.g_ref, bf16[512,384]{1,0:T(8,128)(2,1)} %get-tuple-element.48.refs_0_, ...), custom_call_target="tpu_custom_call" | custom-call | tf_op jit(solution)/shard_map/attend/pallas_call | solution.py:223
  140.9 4.4 %shard_map.67 = bf16[2,8,96,768]{3,2,1,0:T(8,128)(2,1)} custom-call(bf16[8,2,96,256]{3,2,1,0:T(8,128)(2,1)} %get-tuple-element.36.x_ref, bf16[8,2,96,256]{3,2,1,0:T(8,128)(2,1)} %get-tuple-element.51.c_ref, bf16[256,384]{1,0:T(8,128)(2,1)} %get-tuple-element.49.a_ref.refs_1_, bf16[256,384]{1,0:T(8,128)(2,1)} %get-tuple-element.50.b_ref), custom_call_target="tpu_custom_call" | custom-call | tf_op jit(solution)/shard_map/pallas_call | solution.py:309
  145.3 4.7 %collective-permute-done.22.got_ref = bf16[2,8,96,768]{3,2,1,0:T(8,128)(2,1)S(1)} collective-permute-done((bf16[2,8,96,768]{3,2,1,0:T(8,128)(2,1)}, bf16[2,8,96,768]{3,2,1,0:T(8,128)(2,1)S(1)}, u32[]{:S(2)}, u32[]{:S(2)}) %collective-permute-start.22) | collective-permute-done | bytes 2359328 | tf_op jit(solution)/shard_map/ppermute | solution.py:407
  151.5 5.4 %shard_map.68 = (bf16[8,96,768]{2,1,0:T(8,128)(2,1)}, bf16[8,96,768]{2,1,0:T(8,128)(2,1)}) custom-call(bf16[8,2,96,256]{3,2,1,0:T(8,128)(2,1)} %get-tuple-element.35.x_ref, bf16[8,2,96,256]{3,2,1,0:T(8,128)(2,1)} %get-tuple-element.44.c_ref, bf16[256,384]{1,0:T(8,128)(2,1)} %get-tuple-element.49.a_ref.refs_1_, bf16[256,384]{1,0:T(8,128)(2,1)} %get-tuple-element.50.b_ref, ...), custom_call_target="tpu_custom_call" | custom-call | tf_op jit(solution)/shard_map/pallas_call | solution.py:309
  158.7 26.5 %collective-permute-done.23.y_ref = bf16[8,96,768]{2,1,0:T(8,128)(2,1)S(1)} collective-permute-done((bf16[8,96,768]{2,1,0:T(8,128)(2,1)}, bf16[8,96,768]{2,1,0:T(8,128)(2,1)S(1)}, u32[]{:S(2)}, u32[]{:S(2)}) %collective-permute-start.23) | collective-permute-done | bytes 1179680 | tf_op jit(solution)/shard_map/ppermute | solution.py:407
  185.1 3.6 %reduce-scatter.3.cloned.1.call-done.sum_ref = bf16[512,384]{1,0:T(8,128)(2,1)} async-done(((bf16[4096,384]{1,0:T(8,128)(2,1)}), bf16[512,384]{1,0:T(8,128)(2,1)}) %reduce-scatter.3.cloned.1.call-update) | async-done | bytes 393232 | tf_op jit(solution)/shard_map/reduce_scatter | solution.py:468
  188.8 4.8 %shard_map.69 = (bf16[256,384]{1,0:T(8,128)(2,1)}, bf16[256,384]{1,0:T(8,128)(2,1)}, bf16[8,2,96,768]{3,2,1,0:T(8,128)(2,1)}) custom-call(bf16[8,2,96,256]{3,2,1,0:T(8,128)(2,1)} %get-tuple-element.36.x_ref, f32[256,384]{1,0:T(8,128)} %get-tuple-element.53.k_ref, bf16[512,384]{1,0:T(8,128)(2,1)} %reduce-scatter.3.cloned.1.call-done.sum_ref), custom_call_target="tpu_custom_call" | custom-call | tf_op jit(solution)/shard_map/pallas_call | solution.py:309
  193.6 4.7 %collective-permute-done.24.got_ref = bf16[8,2,96,768]{3,2,1,0:T(8,128)(2,1)S(1)} collective-permute-done((bf16[8,2,96,768]{3,2,1,0:T(8,128)(2,1)}, bf16[8,2,96,768]{3,2,1,0:T(8,128)(2,1)S(1)}, u32[]{:S(2)}, u32[]{:S(2)}) %collective-permute-start.24) | collective-permute-done | bytes 2359328 | tf_op jit(solution)/shard_map/ppermute | solution.py:407
  199.8 6.3 %shard_map.70 = bf16[8,288,768]{2,1,0:T(8,128)(2,1)} custom-call(bf16[8,2,96,256]{3,2,1,0:T(8,128)(2,1)} %get-tuple-element.35.x_ref, bf16[256,384]{1,0:T(8,128)(2,1)} %get-tuple-element.61.a_ref.refs_2_, bf16[256,384]{1,0:T(8,128)(2,1)} %get-tuple-element.56.b_ref.refs_3_, bf16[8,2,96,768]{3,2,1,0:T(8,128)(2,1)} %copy-done.7, ...), custom_call_target="tpu_custom_call" | custom-call | tf_op jit(solution)/shard_map/pallas_call | solution.py:309
  206.1 11.0 %inner.1 = (bf16[8,256,384]{2,1,0:T(8,128)(2,1)}, f32[256,128]{1,0:T(8,128)}, f32[256,128]{1,0:T(8,128)}) custom-call(s32[3]{0:T(128)} %pad_add_fusion.me_ref.refs_0_, bf16[256,384]{1,0:T(8,128)(2,1)} %get-tuple-element.49.a_ref.refs_1_, bf16[256,384]{1,0:T(8,128)(2,1)} %get-tuple-element.61.a_ref.refs_2_, bf16[256,384]{1,0:T(8,128)(2,1)} %get-tuple-element.56.b_ref.refs_3_, ...), custom_call_target="tpu_custom_call" | custom-call | tf_op jit(solution)/shard_map/inner/pallas_call | solution.py:379
  222.0 7.3 %all-to-all-start = ((bf16[8,272,384]{2,1,0:T(8,128)(2,1)}), bf16[8,272,384]{2,1,0:T(8,128)(2,1)S(1)}, u32[]{:S(2)}, u32[]{:S(2)}) async-start(bf16[8,272,384]{2,1,0:T(8,128)(2,1)} %pad_maximum_fusion), calls=%async_computation.2 | async-start | bytes 3342336 | tf_op jit(solution)/shard_map/all_to_all | solution.py:497
  229.3 24.0 %all-to-all-done = bf16[8,272,384]{2,1,0:T(8,128)(2,1)S(1)} async-done(((bf16[8,272,384]{2,1,0:T(8,128)(2,1)}), bf16[8,272,384]{2,1,0:T(8,128)(2,1)S(1)}, u32[]{:S(2)}, u32[]{:S(2)}) %all-to-all-start) | async-done | bytes 1671200 | tf_op jit(solution)/shard_map/all_to_all | solution.py:497
  258.6 3.1 %collective-permute-done.25 = bf16[96,768]{1,0:T(8,128)(2,1)S(1)} collective-permute-done((bf16[96,768]{1,0:T(8,128)(2,1)S(1)}, bf16[96,768]{1,0:T(8,128)(2,1)S(1)}, u32[]{:S(2)}, u32[]{:S(2)}) %collective-permute-start.25) | collective-permute-done | bytes 147488 | tf_op jit(solution)/shard_map/ppermute | solution.py:407
  (111 shorter events, 35.0 us)
Async XLA Ops:
  7.2 59.3 %all-gather.3.cloned.1.call-start = ((), (), s32[]{:S(2)}) async-start(), calls=%async_computation.5 | async-start | bytes 1327104 | tf_op jit(solution)/shard_map/all_gather | solution.py:452
  9.7 179.1 %reduce-scatter.3.cloned.1.call-start = ((), (), s32[]{:S(2)}) async-start(), calls=%async_computation.3 | async-start | bytes 3538944 | tf_op jit(solution)/shard_map/reduce_scatter | solution.py:468
  10.7 9.8 %collective-permute-start = (bf16[96,768]{1,0:T(8,128)(2,1)S(1)}, bf16[96,768]{1,0:T(8,128)(2,1)S(1)}, u32[]{:S(2)}, u32[]{:S(2)}) collective-permute-start(bf16[96,768]{1,0:T(8,128)(2,1)S(1)} %bitcast.49), channel_id=1, source_target_pairs={{0,2},{2,0},{1,3},{3,1},{4,6},{6,4},{5,7},{7,5},{8,10},{10,8},{9,1... | collective-permute-start | bytes 442376 | tf_op jit(solution)/shard_map/ppermute | solution.py:407
  20.5 14.3 %collective-permute-start.2 = (bf16[192,768]{1,0:T(8,128)(2,1)S(1)}, bf16[192,768]{1,0:T(8,128)(2,1)S(1)}, u32[]{:S(2)}, u32[]{:S(2)}) collective-permute-start(bf16[192,768]{1,0:T(8,128)(2,1)S(1)} %pad_maximum_fusion.3), channel_id=1, source_target_pairs={{0,224},{32,0},{64,32},{96,64},{128,96},{160,128},{192,160},{224,1... | collective-permute-start | bytes 884744 | tf_op jit(solution)/shard_map/ppermute | solution.py:422
  26.4 13.2 %collective-permute-start.1 = (bf16[192,768]{1,0:T(8,128)(2,1)S(1)}, bf16[192,768]{1,0:T(8,128)(2,1)S(1)}, u32[]{:S(2)}, u32[]{:S(2)}) collective-permute-start(bf16[192,768]{1,0:T(8,128)(2,1)S(1)} %pad_maximum_fusion.3), channel_id=1, source_target_pairs={{0,32},{32,64},{64,96},{96,128},{128,160},{160,192},{192,224},{224... | collective-permute-start | bytes 884744 | tf_op jit(solution)/shard_map/ppermute | solution.py:421
  39.6 12.4 %collective-permute-start.3 = (bf16[192,768]{1,0:T(8,128)(2,1)S(1)}, bf16[192,768]{1,0:T(8,128)(2,1)S(1)}, u32[]{:S(2)}, u32[]{:S(2)}) collective-permute-start(bf16[192,768]{1,0:T(8,128)(2,1)S(1)} %collective-permute-done.1), channel_id=1, source_target_pairs={{0,32},{32,64},{64,96},{96,128},{128,160},{160,192},{192,224},{224... | collective-permute-start | bytes 884744 | tf_op jit(solution)/shard_map/ppermute | solution.py:421
  39.6 12.4 %collective-permute-start.4 = (bf16[192,768]{1,0:T(8,128)(2,1)S(1)}, bf16[192,768]{1,0:T(8,128)(2,1)S(1)}, u32[]{:S(2)}, u32[]{:S(2)}) collective-permute-start(bf16[192,768]{1,0:T(8,128)(2,1)S(1)} %collective-permute-done.2), channel_id=1, source_target_pairs={{0,224},{32,0},{64,32},{96,64},{128,96},{160,128},{192,160},{224,1... | collective-permute-start | bytes 884744 | tf_op jit(solution)/shard_map/ppermute | solution.py:422
  52.0 7.9 %collective-permute-start.6 = (bf16[192,768]{1,0:T(8,128)(2,1)S(1)}, bf16[192,768]{1,0:T(8,128)(2,1)S(1)}, u32[]{:S(2)}, u32[]{:S(2)}) collective-permute-start(bf16[192,768]{1,0:T(8,128)(2,1)S(1)} %collective-permute-done.3), channel_id=1, source_target_pairs={{0,32},{32,64},{64,96},{96,128},{128,160},{160,192},{192,224},{224... | collective-permute-start | bytes 884744 | tf_op jit(solution)/shard_map/ppermute | solution.py:421
  52.0 8.0 %collective-permute-start.7 = (bf16[192,768]{1,0:T(8,128)(2,1)S(1)}, bf16[192,768]{1,0:T(8,128)(2,1)S(1)}, u32[]{:S(2)}, u32[]{:S(2)}) collective-permute-start(bf16[192,768]{1,0:T(8,128)(2,1)S(1)} %collective-permute-done.4), channel_id=1, source_target_pairs={{0,224},{32,0},{64,32},{96,64},{128,96},{160,128},{192,160},{224,1... | collective-permute-start | bytes 884744 | tf_op jit(solution)/shard_map/ppermute | solution.py:422
  55.3 16.7 %copy-start.1 = (bf16[5,192,768]{2,1,0:T(8,128)(2,1)}, bf16[5,192,768]{2,1,0:T(8,128)(2,1)S(1)}, u32[]{:S(2)}) copy-start(bf16[5,192,768]{2,1,0:T(8,128)(2,1)S(1)} %bitcast_dynamic-update-slice_fusion.near_ref.refs_4_) | copy-start | bytes 4423684
  55.3 16.7 %collective-permute-start.5 = (bf16[5,192,768]{2,1,0:T(8,128)(2,1)S(1)}, bf16[5,192,768]{2,1,0:T(8,128)(2,1)}, u32[]{:S(2)}, u32[]{:S(2)}) collective-permute-start(bf16[5,192,768]{2,1,0:T(8,128)(2,1)S(1)} %bitcast_dynamic-update-slice_fusion.near_ref.refs_4_), channel_id=1, source_target_pairs={{0,1},{1,0},{2,3},{3,2},{4,5},{5,4},{6,7},{7,6},{8,9},{9,8},{10,11... | collective-permute-start | bytes 4423688 | tf_op jit(solution)/shard_map/ppermute | solution.py:407
  60.0 6.4 %collective-permute-start.8 = (bf16[96,768]{1,0:T(8,128)(2,1)S(1)}, bf16[96,768]{1,0:T(8,128)(2,1)S(1)}, u32[]{:S(2)}, u32[]{:S(2)}) collective-permute-start(bf16[96,768]{1,0:T(8,128)(2,1)S(1)} %slice.77), channel_id=1, source_target_pairs={{0,32},{32,64},{64,96},{96,128},{128,160},{160,192},{192,224},{224... | collective-permute-start | bytes 442376 | tf_op jit(solution)/shard_map/ppermute | solution.py:426
  60.1 6.3 %collective-permute-start.9 = (bf16[96,768]{1,0:T(8,128)(2,1)S(1)}, bf16[96,768]{1,0:T(8,128)(2,1)S(1)}, u32[]{:S(2)}, u32[]{:S(2)}) collective-permute-start(bf16[96,768]{1,0:T(8,128)(2,1)S(1)} %slice.78), channel_id=1, source_target_pairs={{0,224},{32,0},{64,32},{96,64},{128,96},{160,128},{192,160},{224,1... | collective-permute-start | bytes 442376 | tf_op jit(solution)/shard_map/ppermute | solution.py:427
  66.5 24.8 %collective-permute-start.11 = (bf16[8,96,768]{2,1,0:T(8,128)(2,1)}, bf16[8,96,768]{2,1,0:T(8,128)(2,1)}, u32[]{:S(2)}, u32[]{:S(2)}) collective-permute-start(bf16[8,96,768]{2,1,0:T(8,128)(2,1)} %bitcast.40), channel_id=1, source_target_pairs={{0,2},{2,0},{1,3},{3,1},{4,6},{6,4},{5,7},{7,5},{8,10},{10,8},{9,1... | collective-permute-start | bytes 3538952 | tf_op jit(solution)/shard_map/ppermute | solution.py:407
  68.6 2.5 collective-permute-start.10
  77.7 13.6 %collective-permute-start.15 = (bf16[512,384]{1,0:T(8,128)(2,1)}, bf16[512,384]{1,0:T(8,128)(2,1)S(1)}, u32[]{:S(2)}, u32[]{:S(2)}) collective-permute-start(bf16[512,384]{1,0:T(8,128)(2,1)} %get-tuple-element.48.refs_0_), channel_id=1, source_target_pairs={{0,224},{32,0},{64,32},{96,64},{128,96},{160,128},{192,160},{224,1... | collective-permute-start | bytes 1179656 | tf_op jit(solution)/shard_map/ppermute | solution.py:422
  81.0 13.4 %collective-permute-start.14 = (bf16[512,384]{1,0:T(8,128)(2,1)}, bf16[512,384]{1,0:T(8,128)(2,1)S(1)}, u32[]{:S(2)}, u32[]{:S(2)}) collective-permute-start(bf16[512,384]{1,0:T(8,128)(2,1)} %get-tuple-element.48.refs_0_), channel_id=1, source_target_pairs={{0,32},{32,64},{64,96},{96,128},{128,160},{160,192},{192,224},{224... | collective-permute-start | bytes 1179656 | tf_op jit(solution)/shard_map/ppermute | solution.py:421
  81.0 39.4 %collective-permute-start.12 = (bf16[8,96,768]{2,1,0:T(8,128)(2,1)S(1)}, bf16[8,96,768]{2,1,0:T(8,128)(2,1)S(1)}, u32[]{:S(2)}, u32[]{:S(2)}) collective-permute-start(bf16[8,96,768]{2,1,0:T(8,128)(2,1)S(1)} %bitcast.43), channel_id=1, source_target_pairs={{0,1},{1,0},{2,3},{3,2},{4,5},{5,4},{6,7},{7,6},{8,9},{9,8},{10,11... | collective-permute-start | bytes 3538952 | tf_op jit(solution)/shard_map/ppermute | solution.py:407
  91.3 29.2 %collective-permute-start.13 = (bf16[8,96,768]{2,1,0:T(8,128)(2,1)}, bf16[8,96,768]{2,1,0:T(8,128)(2,1)S(1)}, u32[]{:S(2)}, u32[]{:S(2)}) collective-permute-start(bf16[8,96,768]{2,1,0:T(8,128)(2,1)} %collective-permute-done.11.by_ref.refs_9_), channel_id=1, source_target_pairs={{0,1},{1,0},{2,3},{3,2},{4,5},{5,4},{6,7},{7,6},{8,9},{9,8},{10,11... | collective-permute-start | bytes 3538952 | tf_op jit(solution)/shard_map/ppermute | solution.py:407
  91.3 15.8 %copy-start.11 = (bf16[512,384]{1,0:T(8,128)(2,1)}, bf16[512,384]{1,0:T(8,128)(2,1)S(1)}, u32[]{:S(2)}) copy-start(bf16[512,384]{1,0:T(8,128)(2,1)S(1)} %collective-permute-done.15.refs_2_) | copy-start | bytes 1179652
  91.3 12.1 %collective-permute-start.17 = (bf16[512,384]{1,0:T(8,128)(2,1)S(1)}, bf16[512,384]{1,0:T(8,128)(2,1)S(1)}, u32[]{:S(2)}, u32[]{:S(2)}) collective-permute-start(bf16[512,384]{1,0:T(8,128)(2,1)S(1)} %collective-permute-done.15.refs_2_), channel_id=1, source_target_pairs={{0,224},{32,0},{64,32},{96,64},{128,96},{160,128},{192,160},{224,1... | collective-permute-start | bytes 1179656 | tf_op jit(solution)/shard_map/ppermute | solution.py:422
  94.5 12.7 %collective-permute-start.16 = (bf16[512,384]{1,0:T(8,128)(2,1)S(1)}, bf16[512,384]{1,0:T(8,128)(2,1)S(1)}, u32[]{:S(2)}, u32[]{:S(2)}) collective-permute-start(bf16[512,384]{1,0:T(8,128)(2,1)S(1)} %collective-permute-done.14.refs_1_), channel_id=1, source_target_pairs={{0,32},{32,64},{64,96},{96,128},{128,160},{160,192},{192,224},{224... | collective-permute-start | bytes 1179656 | tf_op jit(solution)/shard_map/ppermute | solution.py:421
  103.4 11.8 %collective-permute-start.19 = (bf16[512,384]{1,0:T(8,128)(2,1)S(1)}, bf16[512,384]{1,0:T(8,128)(2,1)S(1)}, u32[]{:S(2)}, u32[]{:S(2)}) collective-permute-start(bf16[512,384]{1,0:T(8,128)(2,1)S(1)} %collective-permute-done.17.refs_4_), channel_id=1, source_target_pairs={{0,224},{32,0},{64,32},{96,64},{128,96},{160,128},{192,160},{224,1... | collective-permute-start | bytes 1179656 | tf_op jit(solution)/shard_map/ppermute | solution.py:422
  107.1 12.5 %collective-permute-start.18 = (bf16[512,384]{1,0:T(8,128)(2,1)S(1)}, bf16[512,384]{1,0:T(8,128)(2,1)S(1)}, u32[]{:S(2)}, u32[]{:S(2)}) collective-permute-start(bf16[512,384]{1,0:T(8,128)(2,1)S(1)} %collective-permute-done.16.refs_3_), channel_id=1, source_target_pairs={{0,32},{32,64},{64,96},{96,128},{128,160},{160,192},{192,224},{224... | collective-permute-start | bytes 1179656 | tf_op jit(solution)/shard_map/ppermute | solution.py:421
  116.0 13.2 %collective-permute-start.21 = (bf16[256,384]{1,0:T(8,128)(2,1)}, bf16[256,384]{1,0:T(8,128)(2,1)}, u32[]{:S(2)}, u32[]{:S(2)}) collective-permute-start(bf16[256,384]{1,0:T(8,128)(2,1)} %slice.80), channel_id=1, source_target_pairs={{0,224},{32,0},{64,32},{96,64},{128,96},{160,128},{192,160},{224,1... | collective-permute-start | bytes 589832 | tf_op jit(solution)/shard_map/ppermute | solution.py:427
  120.4 8.7 %collective-permute-start.20 = (bf16[256,384]{1,0:T(8,128)(2,1)}, bf16[256,384]{1,0:T(8,128)(2,1)}, u32[]{:S(2)}, u32[]{:S(2)}) collective-permute-start(bf16[256,384]{1,0:T(8,128)(2,1)} %slice.79), channel_id=1, source_target_pairs={{0,32},{32,64},{64,96},{96,128},{128,160},{160,192},{192,224},{224... | collective-permute-start | bytes 589832 | tf_op jit(solution)/shard_map/ppermute | solution.py:426
  140.9 114.6 %reduce-scatter.5.cloned.1.call-start = ((), (), s32[]{:S(2)}) async-start(), calls=%async_computation.4 | async-start | bytes 3981312 | tf_op jit(solution)/shard_map/reduce_scatter | solution.py:485
  145.3 4.7 %collective-permute-start.22 = (bf16[2,8,96,768]{3,2,1,0:T(8,128)(2,1)}, bf16[2,8,96,768]{3,2,1,0:T(8,128)(2,1)S(1)}, u32[]{:S(2)}, u32[]{:S(2)}) collective-permute-start(bf16[2,8,96,768]{3,2,1,0:T(8,128)(2,1)} %shard_map.67), channel_id=1, source_target_pairs={{0,1},{1,0},{2,3},{3,2},{4,5},{5,4},{6,7},{7,6},{8,9},{9,8},{10,11... | collective-permute-start | bytes 7077896 | tf_op jit(solution)/shard_map/ppermute | solution.py:407
  156.9 28.2 %collective-permute-start.23 = (bf16[8,96,768]{2,1,0:T(8,128)(2,1)}, bf16[8,96,768]{2,1,0:T(8,128)(2,1)S(1)}, u32[]{:S(2)}, u32[]{:S(2)}) collective-permute-start(bf16[8,96,768]{2,1,0:T(8,128)(2,1)} %get-tuple-element.52), channel_id=1, source_target_pairs={{0,2},{2,0},{1,3},{3,1},{4,6},{6,4},{5,7},{7,5},{8,10},{10,8},{9,1... | collective-permute-start | bytes 3538952 | tf_op jit(solution)/shard_map/ppermute | solution.py:407
  193.6 4.7 %collective-permute-start.24 = (bf16[8,2,96,768]{3,2,1,0:T(8,128)(2,1)}, bf16[8,2,96,768]{3,2,1,0:T(8,128)(2,1)S(1)}, u32[]{:S(2)}, u32[]{:S(2)}) collective-permute-start(bf16[8,2,96,768]{3,2,1,0:T(8,128)(2,1)} %get-tuple-element.57), channel_id=1, source_target_pairs={{0,1},{1,0},{2,3},{3,2},{4,5},{5,4},{6,7},{7,6},{8,9},{9,8},{10,11... | collective-permute-start | bytes 7077896 | tf_op jit(solution)/shard_map/ppermute | solution.py:407
  222.0 31.3 %all-to-all-start = ((bf16[8,272,384]{2,1,0:T(8,128)(2,1)}), bf16[8,272,384]{2,1,0:T(8,128)(2,1)S(1)}, u32[]{:S(2)}, u32[]{:S(2)}) async-start(bf16[8,272,384]{2,1,0:T(8,128)(2,1)} %pad_maximum_fusion), calls=%async_computation.2 | async-start | bytes 3342336 | tf_op jit(solution)/shard_map/all_to_all | solution.py:497
  256.5 5.2 %collective-permute-start.25 = (bf16[96,768]{1,0:T(8,128)(2,1)S(1)}, bf16[96,768]{1,0:T(8,128)(2,1)S(1)}, u32[]{:S(2)}, u32[]{:S(2)}) collective-permute-start(bf16[96,768]{1,0:T(8,128)(2,1)S(1)} %get-tuple-element.68), channel_id=1, source_target_pairs={{0,2},{2,0},{1,3},{3,1},{4,6},{6,4},{5,7},{7,5},{8,10},{10,8},{9,1... | collective-permute-start | bytes 442376 | tf_op jit(solution)/shard_map/ppermute | solution.py:407
  (14 other events, 78.2 us)
Sparse Core Ops, SparseCore 0:
  10.3 43.4 all-gather.2
  141.0 47.7 reduce-scatter.2
  206.2 48.4 reduce-scatter.4

commit v2 on v0

--- a/solution.py
+++ b/solution.py
@@ -119,32 +119,29 @@
     return (i + 1) // 2 * (1 if i % 2 == 0 else -1)
 
 
-def far_from(i):
-    return lax.div(i + 1, 2) * (1 - 2 * lax.rem(i, 2))
-
-
-def project_kv_body(
-    me_ref, x_ref, near_ref, near_far_ref, far_ref, far_far_ref, k_ref, kl_ref, vl_ref, acc_ref
-):
+def project_kv_body(me_ref, x_ref, near_ref, near_far_ref, far_ref, far_far_ref, k_ref, kl_ref, vl_ref):
     slabs = x_ref.shape[0]
-    width = k_ref.shape[1]
+    rows, width = k_ref.shape
     close = near_ref.shape[0]
-    acc_ref[...] = jnp.zeros_like(acc_ref)
-
-    def take(mine_ref, theirs_ref, first):
-        def step(k, carry):
-            slab = lax.rem(me_ref[0] + slabs + far_from(k + first), slabs)
-            acc_ref[...] += dot(x_ref[slab, 0], mine_ref[k]) + dot(x_ref[slab, 1], theirs_ref[k])
-            return carry
-
-        lax.fori_loop(0, mine_ref.shape[0], step, 0)
-
-    take(near_ref, near_far_ref, 0)
-    take(far_ref, far_far_ref, close)
-    k_ref[...] = acc_ref[:, :width]
-    for at in range(0, width, HD):
-        kl_ref[:, at : at + HD] = normalize(acc_ref[:, at : at + HD])[0].astype(BF)
-    vl_ref[...] = acc_ref[:, width:].astype(BF)
+    for n in range(2 * width // 256):
+        cols = slice(n * 256, (n + 1) * 256)
+        acc = jnp.zeros((rows, 256), F32)
+        for i in range(slabs):
+            slab = lax.rem(me_ref[0] + slabs + distance(i), slabs)
+            if i < close:
+                pieces = near_ref[i, :, cols], near_far_ref[i, :, cols]
+            else:
+                pieces = far_ref[i - close, :, cols], far_far_ref[i - close, :, cols]
+            for c, piece in enumerate(pieces):
+                acc = acc + dot(x_ref[slab, c], piece)
+        for j in range(2):
+            at = n * 256 + j * HD
+            part = acc[:, j * HD : (j + 1) * HD]
+            if at < width:
+                k_ref[:, at : at + HD] = part
+                kl_ref[:, at : at + HD] = normalize(part)[0].astype(BF)
+            else:
+                vl_ref[:, at - width : at - width + HD] = part.astype(BF)
 
 
 def project_kv(me, x, near, near_far, far, far_far):
@@ -157,29 +154,22 @@
             jax.ShapeDtypeStruct((rows, width), BF),
             jax.ShapeDtypeStruct((rows, width), BF),
         ],
-        scratch_shapes=[pltpu.VMEM((rows, 2 * width), F32)],
         name="project_kv",
     )(me, x, near, near_far, far, far_far)
 
 
-def project_qo_body(x_ref, c_ref, b_ref, by_ref, bc_ref, byc_ref, q_ref, g_ref, acc_ref):
+def project_qo_body(x_ref, c_ref, b_ref, by_ref, bc_ref, byc_ref, q_ref, g_ref):
     slabs = x_ref.shape[0]
-    width = q_ref.shape[1]
-    acc_ref[...] = jnp.zeros_like(acc_ref)
-
-    def step(k, carry):
-        for left_ref, at in ((x_ref, 0), (c_ref, width)):
-            cols = slice(at, at + width)
-            part = 0.0
-            for c, (first, second) in enumerate(((b_ref, by_ref), (bc_ref, byc_ref))):
-                piece = jnp.concatenate([first[k, :, cols], second[k, :, cols]], axis=0)
-                part = part + dot(left_ref[k, c], piece)
-            acc_ref[:, cols] += part
-        return carry
-
-    lax.fori_loop(0, slabs, step, 0)
-    q_ref[...] = acc_ref[:, :width]
-    g_ref[...] = acc_ref[:, width:].astype(BF)
+    rows, width = q_ref.shape
+    for left_ref, out_ref, first in ((x_ref, q_ref, 0), (c_ref, g_ref, width)):
+        for at, size in ((0, 256), (256, 128)):
+            cols = slice(first + at, first + at + size)
+            acc = jnp.zeros((rows, size), F32)
+            for k in range(slabs):
+                for c, (one, two) in enumerate(((b_ref, by_ref), (bc_ref, byc_ref))):
+                    piece = jnp.concatenate([one[k, :, cols], two[k, :, cols]], axis=0)
+                    acc = acc + dot(left_ref[k, c], piece)
+            out_ref[:, at : at + size] = acc.astype(out_ref.dtype)
 
 
 VMEM = pl.BlockSpec(memory_space=pltpu.VMEM)
@@ -192,7 +182,6 @@
         project_qo_body,
         in_specs=[VMEM] * 6,
         out_shape=[jax.ShapeDtypeStruct((rows, width), F32), jax.ShapeDtypeStruct((rows, width), BF)],
-        scratch_shapes=[pltpu.VMEM((rows, 2 * width), F32)],
         name="project_qo",
     )(x, c, *pieces)
 
@@ -315,16 +304,30 @@
     terms_of(x_ref, x_ref, kb_ref, vb_ref, store)
 
 
-def key_keep_body(x_ref, a_ref, b_ref, got_ref, stay_ref, y_ref, out_ref):
-    own = x_ref.shape[2]
-
+def key_mine_body(x_ref, a_ref, b_ref, stay_ref, y_ref, part_ref, query_ref):
     def store(r, y, cols, value):
-        total = value + got_ref[r, y, :, cols].astype(F32)
-        out_ref[r, (1 + y) * own : (2 + y) * own, cols] = total.astype(BF)
+        part_ref[r, y, :, cols] = value.astype(BF)
 
     terms_of(x_ref, x_ref, a_ref, b_ref, store)
-    for r in range(x_ref.shape[0]):
-        out_ref[r, :own] = (stay_ref[r].astype(F32) + y_ref[r].astype(F32)).astype(BF)
+
+    def step(r, carry):
+        query_ref[r] = (stay_ref[r].astype(F32) + y_ref[r].astype(F32)).astype(BF)
+        return carry
+
+    lax.fori_loop(0, x_ref.shape[0], step, 0)
+
+
+def key_add_body(part_ref, got_ref, query_ref, out_ref):
+    own = part_ref.shape[2]
+
+    def step(r, carry):
+        out_ref[r, :own] = query_ref[r]
+        for y in range(2):
+            total = part_ref[r, y].astype(F32) + got_ref[r, y].astype(F32)
+            out_ref[r, (1 + y) * own : (2 + y) * own] = total.astype(BF)
+        return carry
+
+    lax.fori_loop(0, part_ref.shape[0], step, 0)
 
 
 def call(body, shapes, *operands):
@@ -475,7 +478,8 @@
     kv_weight = qkv_weight[:, 1:].reshape(own, 2 * width)
     qo_weight = jnp.concatenate([qkv_weight[:, 0], out_weight], axis=1)
     qo_mine = lax.all_gather(qo_weight, "seq")
-    kv_weight = jnp.concatenate([kv_weight, swap(kv_weight, "ylo")], axis=0)
+    kv_y = swap(kv_weight, "ylo")
+    kv_weight = jnp.concatenate([kv_weight, kv_y], axis=0)
     unit, inverse, *turned = prepare(me, tokens[0], cotangent[0], slabs)
     x_keep, x_send, x_r, c_keep, c_send, c_r = turned
     ring, x_r = ring_gather(kv_weight, x_r)
@@ -500,17 +504,20 @@
     key_grad, value_grad, send = call(
         key_send_body, [(row_count, width)] * 2 + [(slabs, 2, own, both)], x_send, key, pair
     )
-    merged = call(
-        key_keep_body,
-        [(slabs, 3 * own, both)],
-        x_keep, key_grad, value_grad, swap(send, "core"), stay, from_y,
-    )[0]
+    got = swap(send, "core")
+    part, query_sum = call(
+        key_mine_body,
+        [(slabs, 2, own, both), (slabs, own, both)],
+        x_keep, key_grad, value_grad, stay, from_y,
+    )
+    merged = call(key_add_body, [(slabs, 3 * own, both)], part, got, query_sum)[0]
     merged, key_grad = lax.optimization_barrier((merged, key_grad))
     merged = lax.psum_scatter(
         merged.reshape(slabs * 3 * own, both), "seq", scatter_dimension=0, tiled=True
     )
     query_out = merged[:own].astype(F32)
-    key_value_grad = merged[own : 2 * own].astype(F32) + swap(merged[2 * own :], "ylo").astype(F32)
+    last = swap(merged[2 * own :], "ylo")
+    key_value_grad = merged[own : 2 * own].astype(F32) + last.astype(F32)
     share, plain, both = inner(
         me, query_back, key_grad, value_grad, near, near_far, far, far_far, qo_pieces, unit
     )
@@ -526,11 +533,11 @@
     totals = jnp.sum(totals, axis=1)[:, :, None] / feature_count
     offset = lax.axis_index(("x", "yhi")) * share.shape[2]
     unit_own = lax.dynamic_slice_in_dim(unit, offset, share.shape[2], 1)
-    branch = (own_share - totals[0] - unit_own * totals[1]) * inverse[:, :1]
+    branch = ((own_share - totals[0] - unit_own * totals[1]) * inverse[:, :1]).astype(BF)
     qkv_grad = jnp.stack(
         [query_out[:, :width], key_value_grad[:, :width], key_value_grad[:, width:]], axis=1
     )
-    return (qkv_grad, query_out[:, width:], branch.astype(BF)[None])
+    return (qkv_grad, query_out[:, width:], branch[None])
 
 
 def solution(mesh):

time: 269 us -> 267 us (level)
  waiting for transfers between devices: 121 us -> 118 us
    pallas_call x4 -> x5, Pallas kernels: 20.7 us -> 25.2 us  [call(): pl.pallas_call(body, in_specs=[VMEM] * len(operands), out_shape=[jax.Shap...]
    ppermute x10, waiting for transfers between devices: 60.2 us -> 55.8 us  [swap(): return lax.ppermute(value, axis, [(0, 1), (1, 0)])]
  transfers between devices with their start and end apart: 36 -> 36, of which waited for: 22 -> 22; matrix products, arithmetic and copies ran while one was open for 4% -> 4% of each run, Pallas kernels for 17% -> 18%
where the time goes in v2:
time: 267 us
  waiting for transfers between devices  118 us (44%)
  Pallas kernels  69.8 us (26%)
  starting transfers between devices  42.9 us (16%)
  between operations  14.1 us (5%)
  other arithmetic  13 us (5%)
  local copies, waits for them, and re-layouts  8.41 us (3%)
    ppermute x10, waiting for transfers between devices, swap(): return lax.ppermute(value, axis, [(0, 1), (1, 0)])  55.8 us
    pallas_call x5, Pallas kernels, call(): pl.pallas_call(body, in_specs=[VMEM] * len(operands), out_shape=[jax.Shap...  25.2 us
    all_to_all x1, waiting for transfers between devices, layer(): load = lax.all_to_all(load, ('x', 'yhi'), 0, 0, tiled=True)  25.1 us
    ppermute x9, waiting for transfers between devices, ring_gather(): high = lax.ppermute(high, 'seq', up)  23.4 us
    ppermute x9, starting transfers between devices, ring_gather(): low = lax.ppermute(low, 'seq', down)  20 us
    pallas_call x1, Pallas kernels, attend(): pl.pallas_call(lambda *refs: attend_body(*refs, count=len(sizes)), grid_s...  11.6 us
    pallas_call x1, Pallas kernels, inner(): pl.pallas_call(lambda *refs: inner_body(*refs, close=close), grid_spec=pl...  10.9 us
    pallas_call x1, Pallas kernels, prepare(): pl.pallas_call(prepare_body, grid_spec=pltpu.PrefetchScalarGridSpec(num_s...  9.86 us
  transfers between devices with their start and end apart: 36, of which 22 were waited for; matrix products, arithmetic and copies ran while one was open for 4% of the time, Pallas kernels for 18%

profile of v2, /device:TPU:16, one launch (start us, length us, event | category | flops | bytes accessed | tf_op | source)
XLA Modules:
  0.0 266.7 jit_solution(9151129836116395610)
XLA Ops:
  12.1 4.3 %collective-permute-done = bf16[96,768]{1,0:T(8,128)(2,1)S(1)} collective-permute-done((bf16[96,768]{1,0:T(8,128)(2,1)S(1)}, bf16[96,768]{1,0:T(8,128)(2,1)S(1)}, u32[]{:S(2)}, u32[]{:S(2)}) %collective-permute-start) | collective-permute-done | bytes 147488 | tf_op jit(solution)/shard_map/ppermute | solution.py:432
  16.4 5.9 %collective-permute-start.2 = (bf16[192,768]{1,0:T(8,128)(2,1)S(1)}, bf16[192,768]{1,0:T(8,128)(2,1)S(1)}, u32[]{:S(2)}, u32[]{:S(2)}) collective-permute-start(bf16[192,768]{1,0:T(8,128)(2,1)S(1)} %constant_dynamic-update-slice_fusion), channel_id=1, source_target_pairs={{0,224},{32,0},{64,32},{96,64},{128,96},{160,128},{192,160},{224,1... | collective-permute-start | bytes 884744 | tf_op jit(solution)/shard_map/ppermute | solution.py:447
  22.9 9.9 %prepare.1 = (f32[256,3072]{1,0:T(8,128)}, f32[256,128]{1,0:T(8,128)}, bf16[8,2,96,256]{3,2,1,0:T(8,128)(2,1)}, bf16[8,2,96,256]{3,2,1,0:T(8,128)(2,1)}, bf16[8,...) custom-call(s32[3]{0:T(128)} %pad_add_fusion.me_ref.refs_0_, ...), custom_call_target="tpu_custom_call" | custom-call | tf_op jit(solution)/shard_map/prepare/pallas_call | solution.py:95
  34.5 3.2 %collective-permute-start.4 = (bf16[192,768]{1,0:T(8,128)(2,1)S(1)}, bf16[192,768]{1,0:T(8,128)(2,1)S(1)}, u32[]{:S(2)}, u32[]{:S(2)}) collective-permute-start(bf16[192,768]{1,0:T(8,128)(2,1)S(1)} %collective-permute-done.2), channel_id=1, source_target_pairs={{0,224},{32,0},{64,32},{96,64},{128,96},{160,128},{192,160},{224,1... | collective-permute-start | bytes 884744 | tf_op jit(solution)/shard_map/ppermute | solution.py:447
  37.8 9.7 %collective-permute-done.3 = bf16[192,768]{1,0:T(8,128)(2,1)} collective-permute-done((bf16[192,768]{1,0:T(8,128)(2,1)S(1)}, bf16[192,768]{1,0:T(8,128)(2,1)}, u32[]{:S(2)}, u32[]{:S(2)}) %collective-permute-start.3) | collective-permute-done | bytes 294944 | tf_op jit(solution)/shard_map/ppermute | solution.py:446
  47.5 3.2 %collective-permute-start.7 = (bf16[192,768]{1,0:T(8,128)(2,1)S(1)}, bf16[192,768]{1,0:T(8,128)(2,1)S(1)}, u32[]{:S(2)}, u32[]{:S(2)}) collective-permute-start(bf16[192,768]{1,0:T(8,128)(2,1)S(1)} %collective-permute-done.4), channel_id=1, source_target_pairs={{0,224},{32,0},{64,32},{96,64},{128,96},{160,128},{192,160},{224,1... | collective-permute-start | bytes 884744 | tf_op jit(solution)/shard_map/ppermute | solution.py:447
  56.2 3.2 %collective-permute-start.9 = (bf16[96,768]{1,0:T(8,128)(2,1)S(1)}, bf16[96,768]{1,0:T(8,128)(2,1)S(1)}, u32[]{:S(2)}, u32[]{:S(2)}) collective-permute-start(bf16[96,768]{1,0:T(8,128)(2,1)S(1)} %slice.70), channel_id=1, source_target_pairs={{0,224},{32,0},{64,32},{96,64},{128,96},{160,128},{192,160},{224,1... | collective-permute-start | bytes 442376 | tf_op jit(solution)/shard_map/ppermute | solution.py:453
  59.4 3.0 %collective-permute-done.8 = bf16[96,768]{1,0:T(8,128)(2,1)S(1)} collective-permute-done((bf16[96,768]{1,0:T(8,128)(2,1)S(1)}, bf16[96,768]{1,0:T(8,128)(2,1)S(1)}, u32[]{:S(2)}, u32[]{:S(2)}) %collective-permute-start.8) | collective-permute-done | bytes 147488 | tf_op jit(solution)/shard_map/ppermute | solution.py:452
  64.3 16.3 %collective-permute-done.11.by_ref.refs_9_ = bf16[8,96,768]{2,1,0:T(8,128)(2,1)} collective-permute-done((bf16[8,96,768]{2,1,0:T(8,128)(2,1)}, bf16[8,96,768]{2,1,0:T(8,128)(2,1)}, u32[]{:S(2)}, u32[]{:S(2)}) %collective-permute-start.11) | collective-permute-done | bytes 1179680 | tf_op jit(solution)/shard_map/ppermute | solution.py:432
  81.6 5.6 %project_kv.1 = (f32[256,384]{1,0:T(8,128)}, bf16[256,384]{1,0:T(8,128)(2,1)}, bf16[256,384]{1,0:T(8,128)(2,1)}) custom-call(s32[3]{0:T(128)} %pad_add_fusion.me_ref.refs_0_, bf16[8,2,256,192]{3,2,1,0:T(8,128)(2,1)} %get-tuple-element.39.x_ref, bf16[5,192,768]{2,1,0:T(8,128)(2,1)} %copy-done.1, ...), custom_call_target="tpu_custom_call" | custom-call | tf_op jit(solution)/shard_map/project_kv/pallas_call | solution.py:149
  90.8 4.3 %collective-permute-done.15.refs_5_ = bf16[256,384]{1,0:T(8,128)(2,1)S(1)} collective-permute-done((bf16[256,384]{1,0:T(8,128)(2,1)}, bf16[256,384]{1,0:T(8,128)(2,1)S(1)}, u32[]{:S(2)}, u32[]{:S(2)}) %collective-permute-start.15) | collective-permute-done | bytes 196640 | tf_op jit(solution)/shard_map/ppermute | solution.py:447
  96.0 2.4 collective-permute-start.17
  99.4 3.4 %collective-permute-done.21.refs_12_ = bf16[256,384]{1,0:T(8,128)(2,1)S(1)} collective-permute-done((bf16[256,384]{1,0:T(8,128)(2,1)}, bf16[256,384]{1,0:T(8,128)(2,1)S(1)}, u32[]{:S(2)}, u32[]{:S(2)}) %collective-permute-start.21) | collective-permute-done | bytes 196640 | tf_op jit(solution)/shard_map/ppermute | solution.py:446
  104.8 2.4 collective-permute-done.16.refs_6_
  108.6 1.9 collective-permute-start.26
  113.1 2.1 collective-permute-done.18.refs_8_
  116.0 3.2 %collective-permute-start.27 = (bf16[256,384]{1,0:T(8,128)(2,1)S(1)}, bf16[256,384]{1,0:T(8,128)(2,1)S(1)}, u32[]{:S(2)}, u32[]{:S(2)}) collective-permute-start(bf16[256,384]{1,0:T(8,128)(2,1)S(1)} %collective-permute-done.26.refs_17_), channel_id=1, source_target_pairs={{0,224},{32,0},{64,32},{96,64},{128,96},{160,128},{192,160},{224,1... | collective-permute-start | bytes 589832 | tf_op jit(solution)/shard_map/ppermute | solution.py:455
  119.2 6.6 %project_qo.1 = (f32[256,384]{1,0:T(8,128)}, bf16[256,384]{1,0:T(8,128)(2,1)}) custom-call(bf16[8,2,256,192]{3,2,1,0:T(8,128)(2,1)} %get-tuple-element.39.x_ref, bf16[8,2,256,192]{3,2,1,0:T(8,128)(2,1)} %get-tuple-element.44.c_ref, bf16[8,96,768]{2,1,0:T(8,128)(2,1)} %bitcast.41, bf16[8,96,768]{2,1,0:T(8,128)(2,1)} %collective-permute-done.11.by_ref.refs_9_, ...), custom_call_target="tpu_custom_call" | custom-call | tf_op jit(solution)/shard_map/project_qo/pallas_call | solution.py:181
  127.2 11.6 %attend.1 = (bf16[256,384]{1,0:T(8,128)(2,1)}, bf16[256,384]{1,0:T(8,128)(2,1)}, bf16[8,2,256,384]{3,2,1,0:T(8,128)(2,1)}) custom-call(s32[3]{0:T(128)} %pad_add_fusion.me_ref.refs_0_, f32[256,384]{1,0:T(8,128)} %get-tuple-element.45.refs_1_, bf16[256,384]{1,0:T(8,128)(2,1)} %get-tuple-element.46.refs_2_, bf16[256,384]{1,0:T(8,128)(2,1)} %get-tuple-element.47.refs_3_, ...), custom_call_target="tpu_custom_call" | custom-call | tf_op jit(solution)/shard_map/attend/pallas_call | solution.py:234
  138.9 4.4 %shard_map.67 = bf16[2,8,96,768]{3,2,1,0:T(8,128)(2,1)} custom-call(bf16[8,2,96,256]{3,2,1,0:T(8,128)(2,1)} %get-tuple-element.37.x_ref, bf16[8,2,96,256]{3,2,1,0:T(8,128)(2,1)} %get-tuple-element.51.c_ref, bf16[256,384]{1,0:T(8,128)(2,1)} %get-tuple-element.49.a_ref.refs_1_, bf16[256,384]{1,0:T(8,128)(2,1)} %get-tuple-element.50.b_ref), custom_call_target="tpu_custom_call" | custom-call | tf_op jit(solution)/shard_map/pallas_call | solution.py:334
  143.3 4.7 %collective-permute-done.28.got_ref = bf16[2,8,96,768]{3,2,1,0:T(8,128)(2,1)S(1)} collective-permute-done((bf16[2,8,96,768]{3,2,1,0:T(8,128)(2,1)}, bf16[2,8,96,768]{3,2,1,0:T(8,128)(2,1)S(1)}, u32[]{:S(2)}, u32[]{:S(2)}) %collective-permute-start.28) | collective-permute-done | bytes 2359328 | tf_op jit(solution)/shard_map/ppermute | solution.py:432
  149.6 5.1 %shard_map.68 = (bf16[8,96,768]{2,1,0:T(8,128)(2,1)}, bf16[8,96,768]{2,1,0:T(8,128)(2,1)}) custom-call(bf16[8,2,96,256]{3,2,1,0:T(8,128)(2,1)} %get-tuple-element.36.x_ref, bf16[8,2,96,256]{3,2,1,0:T(8,128)(2,1)} %get-tuple-element.43.c_ref, bf16[256,384]{1,0:T(8,128)(2,1)} %get-tuple-element.49.a_ref.refs_1_, bf16[256,384]{1,0:T(8,128)(2,1)} %get-tuple-element.50.b_ref, ...), custom_call_target="tpu_custom_call" | custom-call | tf_op jit(solution)/shard_map/pallas_call | solution.py:334
  155.9 27.1 %collective-permute-done.29.y_ref = bf16[8,96,768]{2,1,0:T(8,128)(2,1)S(1)} collective-permute-done((bf16[8,96,768]{2,1,0:T(8,128)(2,1)}, bf16[8,96,768]{2,1,0:T(8,128)(2,1)S(1)}, u32[]{:S(2)}, u32[]{:S(2)}) %collective-permute-start.29) | collective-permute-done | bytes 1179680 | tf_op jit(solution)/shard_map/ppermute | solution.py:432
  184.4 4.8 %shard_map.69 = (bf16[256,384]{1,0:T(8,128)(2,1)}, bf16[256,384]{1,0:T(8,128)(2,1)}, bf16[8,2,96,768]{3,2,1,0:T(8,128)(2,1)}) custom-call(bf16[8,2,96,256]{3,2,1,0:T(8,128)(2,1)} %get-tuple-element.37.x_ref, f32[256,384]{1,0:T(8,128)} %get-tuple-element.53.k_ref, bf16[512,384]{1,0:T(8,128)(2,1)} %reduce-scatter.3.cloned.1.call-done.sum_ref), custom_call_target="tpu_custom_call" | custom-call | tf_op jit(solution)/shard_map/pallas_call | solution.py:334
  189.3 5.7 %shard_map.70 = (bf16[8,2,96,768]{3,2,1,0:T(8,128)(2,1)}, bf16[8,96,768]{2,1,0:T(8,128)(2,1)}) custom-call(bf16[8,2,96,256]{3,2,1,0:T(8,128)(2,1)} %get-tuple-element.36.x_ref, bf16[256,384]{1,0:T(8,128)(2,1)} %get-tuple-element.63.a_ref.refs_2_, bf16[256,384]{1,0:T(8,128)(2,1)} %get-tuple-element.56.b_ref.refs_3_, ...), custom_call_target="tpu_custom_call" | custom-call | tf_op jit(solution)/shard_map/pallas_call | solution.py:334
  196.4 5.1 %shard_map.71 = bf16[8,288,768]{2,1,0:T(8,128)(2,1)} custom-call(bf16[8,2,96,768]{3,2,1,0:T(8,128)(2,1)} %get-tuple-element.59.part_ref, bf16[8,2,96,768]{3,2,1,0:T(8,128)(2,1)} %copy-done.5, bf16[8,96,768]{2,1,0:T(8,128)(2,1)} %get-tuple-element.61.query_ref), custom_call_target="tpu_custom_call" | custom-call | tf_op jit(solution)/shard_map/pallas_call | solution.py:334
  201.5 10.9 %inner.1 = (bf16[8,256,384]{2,1,0:T(8,128)(2,1)}, f32[256,128]{1,0:T(8,128)}, f32[256,128]{1,0:T(8,128)}) custom-call(s32[3]{0:T(128)} %pad_add_fusion.me_ref.refs_0_, bf16[256,384]{1,0:T(8,128)(2,1)} %get-tuple-element.49.a_ref.refs_1_, bf16[256,384]{1,0:T(8,128)(2,1)} %get-tuple-element.63.a_ref.refs_2_, bf16[256,384]{1,0:T(8,128)(2,1)} %get-tuple-element.56.b_ref.refs_3_, ...), custom_call_target="tpu_custom_call" | custom-call | tf_op jit(solution)/shard_map/inner/pallas_call | solution.py:404
  214.6 2.8 %pad_maximum_fusion = bf16[8,272,384]{2,1,0:T(8,128)(2,1)} fusion(bf16[8,16,384]{2,1,0:T(8,128)(2,1)S(1)} %broadcast_in_dim.7, bf16[8,256,384]{2,1,0:T(8,128)(2,1)} %get-tuple-element.65), kind=kLoop, calls=%fused_computation.1 | loop fusion | flops 3342336 | bytes 3342336 | tf_op jit(solution)/shard_map/concatenate | solution.py:527
  217.4 7.4 %all-to-all-start = ((bf16[8,272,384]{2,1,0:T(8,128)(2,1)}), bf16[8,272,384]{2,1,0:T(8,128)(2,1)S(1)}, u32[]{:S(2)}, u32[]{:S(2)}) async-start(bf16[8,272,384]{2,1,0:T(8,128)(2,1)} %pad_maximum_fusion), calls=%async_computation.2 | async-start | bytes 3342336 | tf_op jit(solution)/shard_map/all_to_all | solution.py:528
  224.9 25.1 %all-to-all-done = bf16[8,272,384]{2,1,0:T(8,128)(2,1)S(1)} async-done(((bf16[8,272,384]{2,1,0:T(8,128)(2,1)}), bf16[8,272,384]{2,1,0:T(8,128)(2,1)S(1)}, u32[]{:S(2)}, u32[]{:S(2)}) %all-to-all-start) | async-done | bytes 1671200 | tf_op jit(solution)/shard_map/all_to_all | solution.py:528
  250.3 1.9 fusion.3
  255.1 3.3 %collective-permute-done.31 = bf16[96,768]{1,0:T(8,128)(2,1)S(1)} collective-permute-done((bf16[96,768]{1,0:T(8,128)(2,1)S(1)}, bf16[96,768]{1,0:T(8,128)(2,1)S(1)}, u32[]{:S(2)}, u32[]{:S(2)}) %collective-permute-start.31) | collective-permute-done | bytes 147488 | tf_op jit(solution)/shard_map/ppermute | solution.py:432
  (136 shorter events, 41.8 us)
Async XLA Ops:
  7.2 46.3 %all-gather.3.cloned.1.call-start = ((), (), s32[]{:S(2)}) async-start(), calls=%async_computation.5 | async-start | bytes 1327104 | tf_op jit(solution)/shard_map/all_gather | solution.py:480
  9.7 174.8 %reduce-scatter.3.cloned.1.call-start = ((), (), s32[]{:S(2)}) async-start(), calls=%async_computation.3 | async-start | bytes 3538944 | tf_op jit(solution)/shard_map/reduce_scatter | solution.py:496
  16.4 16.4 %collective-permute-start.2 = (bf16[192,768]{1,0:T(8,128)(2,1)S(1)}, bf16[192,768]{1,0:T(8,128)(2,1)S(1)}, u32[]{:S(2)}, u32[]{:S(2)}) collective-permute-start(bf16[192,768]{1,0:T(8,128)(2,1)S(1)} %constant_dynamic-update-slice_fusion), channel_id=1, source_target_pairs={{0,224},{32,0},{64,32},{96,64},{128,96},{160,128},{192,160},{224,1... | collective-permute-start | bytes 884744 | tf_op jit(solution)/shard_map/ppermute | solution.py:447
  22.3 12.2 %collective-permute-start.1 = (bf16[192,768]{1,0:T(8,128)(2,1)S(1)}, bf16[192,768]{1,0:T(8,128)(2,1)S(1)}, u32[]{:S(2)}, u32[]{:S(2)}) collective-permute-start(bf16[192,768]{1,0:T(8,128)(2,1)S(1)} %constant_dynamic-update-slice_fusion), channel_id=1, source_target_pairs={{0,32},{32,64},{64,96},{96,128},{128,160},{160,192},{192,224},{224... | collective-permute-start | bytes 884744 | tf_op jit(solution)/shard_map/ppermute | solution.py:446
  34.5 13.0 %collective-permute-start.3 = (bf16[192,768]{1,0:T(8,128)(2,1)S(1)}, bf16[192,768]{1,0:T(8,128)(2,1)}, u32[]{:S(2)}, u32[]{:S(2)}) collective-permute-start(bf16[192,768]{1,0:T(8,128)(2,1)S(1)} %collective-permute-done.1), channel_id=1, source_target_pairs={{0,32},{32,64},{64,96},{96,128},{128,160},{160,192},{192,224},{224... | collective-permute-start | bytes 884744 | tf_op jit(solution)/shard_map/ppermute | solution.py:446
  34.5 13.0 %collective-permute-start.4 = (bf16[192,768]{1,0:T(8,128)(2,1)S(1)}, bf16[192,768]{1,0:T(8,128)(2,1)S(1)}, u32[]{:S(2)}, u32[]{:S(2)}) collective-permute-start(bf16[192,768]{1,0:T(8,128)(2,1)S(1)} %collective-permute-done.2), channel_id=1, source_target_pairs={{0,224},{32,0},{64,32},{96,64},{128,96},{160,128},{192,160},{224,1... | collective-permute-start | bytes 884744 | tf_op jit(solution)/shard_map/ppermute | solution.py:447
  47.5 8.5 %collective-permute-start.6 = (bf16[192,768]{1,0:T(8,128)(2,1)}, bf16[192,768]{1,0:T(8,128)(2,1)S(1)}, u32[]{:S(2)}, u32[]{:S(2)}) collective-permute-start(bf16[192,768]{1,0:T(8,128)(2,1)} %collective-permute-done.3), channel_id=1, source_target_pairs={{0,32},{32,64},{64,96},{96,128},{128,160},{160,192},{192,224},{224... | collective-permute-start | bytes 884744 | tf_op jit(solution)/shard_map/ppermute | solution.py:446
  47.5 8.6 %collective-permute-start.7 = (bf16[192,768]{1,0:T(8,128)(2,1)S(1)}, bf16[192,768]{1,0:T(8,128)(2,1)S(1)}, u32[]{:S(2)}, u32[]{:S(2)}) collective-permute-start(bf16[192,768]{1,0:T(8,128)(2,1)S(1)} %collective-permute-done.4), channel_id=1, source_target_pairs={{0,224},{32,0},{64,32},{96,64},{128,96},{160,128},{192,160},{224,1... | collective-permute-start | bytes 884744 | tf_op jit(solution)/shard_map/ppermute | solution.py:447
  51.8 29.7 %collective-permute-start.5 = (bf16[5,192,768]{2,1,0:T(8,128)(2,1)S(1)}, bf16[5,192,768]{2,1,0:T(8,128)(2,1)}, u32[]{:S(2)}, u32[]{:S(2)}) collective-permute-start(bf16[5,192,768]{2,1,0:T(8,128)(2,1)S(1)} %bitcast_dynamic-update-slice_fusion.near_ref.refs_4_), channel_id=1, source_target_pairs={{0,1},{1,0},{2,3},{3,2},{4,5},{5,4},{6,7},{7,6},{8,9},{9,8},{10,11... | collective-permute-start | bytes 4423688 | tf_op jit(solution)/shard_map/ppermute | solution.py:432
  53.5 27.1 %collective-permute-start.11 = (bf16[8,96,768]{2,1,0:T(8,128)(2,1)}, bf16[8,96,768]{2,1,0:T(8,128)(2,1)}, u32[]{:S(2)}, u32[]{:S(2)}) collective-permute-start(bf16[8,96,768]{2,1,0:T(8,128)(2,1)} %bitcast.40), channel_id=1, source_target_pairs={{0,2},{2,0},{1,3},{3,1},{4,6},{6,4},{5,7},{7,5},{8,10},{10,8},{9,1... | collective-permute-start | bytes 3538952 | tf_op jit(solution)/shard_map/ppermute | solution.py:432
  56.0 6.4 %collective-permute-start.8 = (bf16[96,768]{1,0:T(8,128)(2,1)S(1)}, bf16[96,768]{1,0:T(8,128)(2,1)S(1)}, u32[]{:S(2)}, u32[]{:S(2)}) collective-permute-start(bf16[96,768]{1,0:T(8,128)(2,1)S(1)} %slice.69), channel_id=1, source_target_pairs={{0,32},{32,64},{64,96},{96,128},{128,160},{160,192},{192,224},{224... | collective-permute-start | bytes 442376 | tf_op jit(solution)/shard_map/ppermute | solution.py:452
  56.2 6.3 %collective-permute-start.9 = (bf16[96,768]{1,0:T(8,128)(2,1)S(1)}, bf16[96,768]{1,0:T(8,128)(2,1)S(1)}, u32[]{:S(2)}, u32[]{:S(2)}) collective-permute-start(bf16[96,768]{1,0:T(8,128)(2,1)S(1)} %slice.70), channel_id=1, source_target_pairs={{0,224},{32,0},{64,32},{96,64},{128,96},{160,128},{192,160},{224,1... | collective-permute-start | bytes 442376 | tf_op jit(solution)/shard_map/ppermute | solution.py:453
  63.7 16.9 %collective-permute-start.10 = (bf16[3,192,768]{2,1,0:T(8,128)(2,1)S(1)}, bf16[3,192,768]{2,1,0:T(8,128)(2,1)S(1)}, u32[]{:S(2)}, u32[]{:S(2)}) collective-permute-start(bf16[3,192,768]{2,1,0:T(8,128)(2,1)S(1)} %pad_maximum_fusion.1.far_ref.refs_6_), channel_id=1, source_target_pairs={{0,1},{1,0},{2,3},{3,2},{4,5},{5,4},{6,7},{7,6},{8,9},{9,8},{10,11... | collective-permute-start | bytes 2654216 | tf_op jit(solution)/shard_map/ppermute | solution.py:432
  63.8 52.2 %collective-permute-start.12 = (bf16[8,96,768]{2,1,0:T(8,128)(2,1)S(1)}, bf16[8,96,768]{2,1,0:T(8,128)(2,1)}, u32[]{:S(2)}, u32[]{:S(2)}) collective-permute-start(bf16[8,96,768]{2,1,0:T(8,128)(2,1)S(1)} %bitcast.43), channel_id=1, source_target_pairs={{0,1},{1,0},{2,3},{3,2},{4,5},{5,4},{6,7},{7,6},{8,9},{9,8},{10,11... | collective-permute-start | bytes 3538952 | tf_op jit(solution)/shard_map/ppermute | solution.py:432
  80.6 38.6 %collective-permute-start.13 = (bf16[8,96,768]{2,1,0:T(8,128)(2,1)}, bf16[8,96,768]{2,1,0:T(8,128)(2,1)}, u32[]{:S(2)}, u32[]{:S(2)}) collective-permute-start(bf16[8,96,768]{2,1,0:T(8,128)(2,1)} %collective-permute-done.11.by_ref.refs_9_), channel_id=1, source_target_pairs={{0,1},{1,0},{2,3},{3,2},{4,5},{5,4},{6,7},{7,6},{8,9},{9,8},{10,11... | collective-permute-start | bytes 3538952 | tf_op jit(solution)/shard_map/ppermute | solution.py:432
  87.2 8.0 %collective-permute-start.15 = (bf16[256,384]{1,0:T(8,128)(2,1)}, bf16[256,384]{1,0:T(8,128)(2,1)S(1)}, u32[]{:S(2)}, u32[]{:S(2)}) collective-permute-start(bf16[256,384]{1,0:T(8,128)(2,1)} %get-tuple-element.47.refs_3_), channel_id=1, source_target_pairs={{0,224},{32,0},{64,32},{96,64},{128,96},{160,128},{192,160},{224,1... | collective-permute-start | bytes 589832 | tf_op jit(solution)/shard_map/ppermute | solution.py:447
  87.6 8.5 %collective-permute-start.14 = (bf16[256,384]{1,0:T(8,128)(2,1)}, bf16[256,384]{1,0:T(8,128)(2,1)S(1)}, u32[]{:S(2)}, u32[]{:S(2)}) collective-permute-start(bf16[256,384]{1,0:T(8,128)(2,1)} %get-tuple-element.47.refs_3_), channel_id=1, source_target_pairs={{0,32},{32,64},{64,96},{96,128},{128,160},{160,192},{192,224},{224... | collective-permute-start | bytes 589832 | tf_op jit(solution)/shard_map/ppermute | solution.py:446
  89.2 10.2 %collective-permute-start.22 = (bf16[256,384]{1,0:T(8,128)(2,1)}, bf16[256,384]{1,0:T(8,128)(2,1)S(1)}, u32[]{:S(2)}, u32[]{:S(2)}) collective-permute-start(bf16[256,384]{1,0:T(8,128)(2,1)} %get-tuple-element.48.refs_11_), channel_id=1, source_target_pairs={{0,224},{32,0},{64,32},{96,64},{128,96},{160,128},{192,160},{224,1... | collective-permute-start | bytes 589832 | tf_op jit(solution)/shard_map/ppermute | solution.py:447
  95.2 7.6 %collective-permute-start.21 = (bf16[256,384]{1,0:T(8,128)(2,1)}, bf16[256,384]{1,0:T(8,128)(2,1)S(1)}, u32[]{:S(2)}, u32[]{:S(2)}) collective-permute-start(bf16[256,384]{1,0:T(8,128)(2,1)} %get-tuple-element.48.refs_11_), channel_id=1, source_target_pairs={{0,32},{32,64},{64,96},{96,128},{128,160},{160,192},{192,224},{224... | collective-permute-start | bytes 589832 | tf_op jit(solution)/shard_map/ppermute | solution.py:446
  96.0 7.2 %collective-permute-start.17 = (bf16[256,384]{1,0:T(8,128)(2,1)S(1)}, bf16[256,384]{1,0:T(8,128)(2,1)S(1)}, u32[]{:S(2)}, u32[]{:S(2)}) collective-permute-start(bf16[256,384]{1,0:T(8,128)(2,1)S(1)} %collective-permute-done.15.refs_5_), channel_id=1, source_target_pairs={{0,224},{32,0},{64,32},{96,64},{128,96},{160,128},{192,160},{224,1... | collective-permute-start | bytes 589832 | tf_op jit(solution)/shard_map/ppermute | solution.py:447
  99.4 7.9 %collective-permute-start.16 = (bf16[256,384]{1,0:T(8,128)(2,1)S(1)}, bf16[256,384]{1,0:T(8,128)(2,1)S(1)}, u32[]{:S(2)}, u32[]{:S(2)}) collective-permute-start(bf16[256,384]{1,0:T(8,128)(2,1)S(1)} %collective-permute-done.14.refs_4_), channel_id=1, source_target_pairs={{0,32},{32,64},{64,96},{96,128},{128,160},{160,192},{192,224},{224... | collective-permute-start | bytes 589832 | tf_op jit(solution)/shard_map/ppermute | solution.py:446
  102.8 5.8 %collective-permute-start.24 = (bf16[256,384]{1,0:T(8,128)(2,1)S(1)}, bf16[256,384]{1,0:T(8,128)(2,1)S(1)}, u32[]{:S(2)}, u32[]{:S(2)}) collective-permute-start(bf16[256,384]{1,0:T(8,128)(2,1)S(1)} %collective-permute-done.22.refs_13_), channel_id=1, source_target_pairs={{0,224},{32,0},{64,32},{96,64},{128,96},{160,128},{192,160},{224,1... | collective-permute-start | bytes 589832 | tf_op jit(solution)/shard_map/ppermute | solution.py:447
  103.2 9.0 %collective-permute-start.23 = (bf16[256,384]{1,0:T(8,128)(2,1)S(1)}, bf16[256,384]{1,0:T(8,128)(2,1)S(1)}, u32[]{:S(2)}, u32[]{:S(2)}) collective-permute-start(bf16[256,384]{1,0:T(8,128)(2,1)S(1)} %collective-permute-done.21.refs_12_), channel_id=1, source_target_pairs={{0,32},{32,64},{64,96},{96,128},{128,160},{160,192},{192,224},{224... | collective-permute-start | bytes 589832 | tf_op jit(solution)/shard_map/ppermute | solution.py:446
  107.2 8.0 %collective-permute-start.18 = (bf16[256,384]{1,0:T(8,128)(2,1)S(1)}, bf16[256,384]{1,0:T(8,128)(2,1)S(1)}, u32[]{:S(2)}, u32[]{:S(2)}) collective-permute-start(bf16[256,384]{1,0:T(8,128)(2,1)S(1)} %collective-permute-done.16.refs_6_), channel_id=1, source_target_pairs={{0,32},{32,64},{64,96},{96,128},{128,160},{160,192},{192,224},{224... | collective-permute-start | bytes 589832 | tf_op jit(solution)/shard_map/ppermute | solution.py:446
  108.6 7.4 %collective-permute-start.26 = (bf16[256,384]{1,0:T(8,128)(2,1)S(1)}, bf16[256,384]{1,0:T(8,128)(2,1)S(1)}, u32[]{:S(2)}, u32[]{:S(2)}) collective-permute-start(bf16[256,384]{1,0:T(8,128)(2,1)S(1)} %collective-permute-done.24.refs_15_), channel_id=1, source_target_pairs={{0,224},{32,0},{64,32},{96,64},{128,96},{160,128},{192,160},{224,1... | collective-permute-start | bytes 589832 | tf_op jit(solution)/shard_map/ppermute | solution.py:447
  112.2 13.7 %collective-permute-start.19 = (bf16[256,384]{1,0:T(8,128)(2,1)S(1)}, bf16[256,384]{1,0:T(8,128)(2,1)S(1)}, u32[]{:S(2)}, u32[]{:S(2)}) collective-permute-start(bf16[256,384]{1,0:T(8,128)(2,1)S(1)} %collective-permute-done.17.refs_7_), channel_id=1, source_target_pairs={{0,224},{32,0},{64,32},{96,64},{128,96},{160,128},{192,160},{224,1... | collective-permute-start | bytes 589832 | tf_op jit(solution)/shard_map/ppermute | solution.py:447
  115.2 10.6 %collective-permute-start.25 = (bf16[256,384]{1,0:T(8,128)(2,1)S(1)}, bf16[256,384]{1,0:T(8,128)(2,1)S(1)}, u32[]{:S(2)}, u32[]{:S(2)}) collective-permute-start(bf16[256,384]{1,0:T(8,128)(2,1)S(1)} %collective-permute-done.23.refs_14_), channel_id=1, source_target_pairs={{0,32},{32,64},{64,96},{96,128},{128,160},{160,192},{192,224},{224... | collective-permute-start | bytes 589832 | tf_op jit(solution)/shard_map/ppermute | solution.py:446
  116.0 10.5 %collective-permute-start.20 = (bf16[256,384]{1,0:T(8,128)(2,1)S(1)}, bf16[256,384]{1,0:T(8,128)(2,1)}, u32[]{:S(2)}, u32[]{:S(2)}) collective-permute-start(bf16[256,384]{1,0:T(8,128)(2,1)S(1)} %collective-permute-done.18.refs_8_), channel_id=1, source_target_pairs={{0,32},{32,64},{64,96},{96,128},{128,160},{160,192},{192,224},{224... | collective-permute-start | bytes 589832 | tf_op jit(solution)/shard_map/ppermute | solution.py:455
  116.0 10.5 %collective-permute-start.27 = (bf16[256,384]{1,0:T(8,128)(2,1)S(1)}, bf16[256,384]{1,0:T(8,128)(2,1)S(1)}, u32[]{:S(2)}, u32[]{:S(2)}) collective-permute-start(bf16[256,384]{1,0:T(8,128)(2,1)S(1)} %collective-permute-done.26.refs_17_), channel_id=1, source_target_pairs={{0,224},{32,0},{64,32},{96,64},{128,96},{160,128},{192,160},{224,1... | collective-permute-start | bytes 589832 | tf_op jit(solution)/shard_map/ppermute | solution.py:455
  138.9 113.3 %reduce-scatter.5.cloned.1.call-start = ((), (), s32[]{:S(2)}) async-start(), calls=%async_computation.4 | async-start | bytes 3981312 | tf_op jit(solution)/shard_map/reduce_scatter | solution.py:515
  154.7 28.2 %collective-permute-start.29 = (bf16[8,96,768]{2,1,0:T(8,128)(2,1)}, bf16[8,96,768]{2,1,0:T(8,128)(2,1)S(1)}, u32[]{:S(2)}, u32[]{:S(2)}) collective-permute-start(bf16[8,96,768]{2,1,0:T(8,128)(2,1)} %get-tuple-element.52), channel_id=1, source_target_pairs={{0,2},{2,0},{1,3},{3,1},{4,6},{6,4},{5,7},{7,5},{8,10},{10,8},{9,1... | collective-permute-start | bytes 3538952 | tf_op jit(solution)/shard_map/ppermute | solution.py:432
  217.4 32.6 %all-to-all-start = ((bf16[8,272,384]{2,1,0:T(8,128)(2,1)}), bf16[8,272,384]{2,1,0:T(8,128)(2,1)S(1)}, u32[]{:S(2)}, u32[]{:S(2)}) async-start(bf16[8,272,384]{2,1,0:T(8,128)(2,1)} %pad_maximum_fusion), calls=%async_computation.2 | async-start | bytes 3342336 | tf_op jit(solution)/shard_map/all_to_all | solution.py:528
  (27 other events, 314.0 us)
Sparse Core Ops, SparseCore 0:
  10.3 43.1 all-gather.2
  139.0 45.4 reduce-scatter.2
  201.6 48.5 reduce-scatter.4
